TPU v7x, 32 devices: a whole 2x2x4 slice. The times are simulated.
32 devices in a mesh: tp: 4 (over z), ep: 8 (over y, x, core).
Axes of the slice: x: 2, y: 2, z: 4, core: 2. Of those that a mesh axis runs over, the one named last changes fastest.
Arguments:
- tokens: bfloat16 [3072, 2048], P('ep', 'tp'), may hold values from -6 to 6
- norm_gain: float32 [2048], replicated, may hold values from 0.25 to 1.75
- shared_gate: bfloat16 [2048, 2816], P('ep', 'tp'), may hold values from -0.125 to 0.125
- shared_up: bfloat16 [2048, 2816], P('ep', 'tp'), may hold values from -0.125 to 0.125
- shared_down: bfloat16 [2816, 2048], P('tp', 'ep'), may hold values from -0.15625 to 0.15625
- expert_gate: bfloat16 [4, 8, 704, 2048], P('tp', 'ep'), may hold values from -0.125 to 0.125
- expert_up: bfloat16 [4, 8, 704, 2048], P('tp', 'ep'), may hold values from -0.125 to 0.125
- expert_down: bfloat16 [16, 1408, 2048], P('ep', None, 'tp'), may hold values from -0.15625 to 0.15625
- chosen: int32 [16, 384], P('ep'), may hold values from 0 to 3071, as said below
- gates: float32 [16, 384], P('ep'), may hold values from 0.1 to 1
Outputs:
- mixed: bfloat16 [3072, 2048], P('ep', 'tp')
Inputs may be any that keep to these rules, and one draw needn't show every extreme that they name: Each row of chosen holds 384 different token indices in rising order. Of one row, at most 96 lie among the 384 tokens of one index of ep (tokens s * 384 to (s + 1) * 384 - 1), and in every row exactly 96 lie among those of some index.
All inputs are finite; a program needn't handle non-finite values.
Results may differ from a plain program's by a relative error of at most 0.012.
Values may be sent and summed in bfloat16 or wider, within the bound.
A program may use at most 64 MiB of HBM per device.

v0:
```python
import jax
import jax.numpy as jnp
from jax import lax
from jax.sharding import PartitionSpec as P

EXP_DEV = 2
TOK_DEV = 384
CAP = 384


norm_eps = 1e-06


def on_device(
    tokens,
    norm_gain,
    shared_gate,
    shared_up,
    shared_down,
    expert_gate,
    expert_up,
    expert_down,
    chosen,
    gates,
):
    tp_count = lax.axis_size("tp")
    ep_count = lax.axis_size("ep")
    slice_width = tokens.shape[1]
    whole = lax.all_gather(tokens, "tp", axis=1, tiled=True)
    widened = whole.astype(jnp.float32)
    inv_scale = lax.rsqrt(jnp.mean(widened * widened, axis=1, keepdims=True) + norm_eps)
    normed = (widened * inv_scale * norm_gain).astype(jnp.bfloat16)
    gate_sum = jnp.dot(
        normed,
        lax.all_gather(shared_gate, "ep", axis=0, tiled=True),
        preferred_element_type=jnp.float32,
    )
    up_sum = jnp.dot(
        normed,
        lax.all_gather(shared_up, "ep", axis=0, tiled=True),
        preferred_element_type=jnp.float32,
    )
    shared_hidden = (jax.nn.silu(gate_sum) * up_sum).astype(jnp.bfloat16)
    partial_out = jnp.dot(
        shared_hidden,
        lax.all_gather(shared_down, "ep", axis=1, tiled=True),
        preferred_element_type=jnp.float32,
    )
    shared_part = lax.psum_scatter(partial_out, "tp", scatter_dimension=1, tiled=True)
    slot_most = 2 * CAP // ep_count
    slot_count = ep_count * slot_most
    sources = chosen // TOK_DEV
    source_flags = (
        sources[:, :, None] == jnp.arange(ep_count, dtype=jnp.int32)[None, None, :]
    ).astype(jnp.int32)
    counts = jnp.sum(source_flags, axis=1)
    starts = jnp.cumsum(counts, axis=1) - counts
    run_start = jnp.take_along_axis(starts, sources, axis=1)
    slot_index = sources * slot_most + jnp.arange(CAP, dtype=jnp.int32)[None, :] - run_start
    local_ids = chosen - sources * TOK_DEV
    expert_rows = jnp.arange(EXP_DEV, dtype=jnp.int32)[:, None]
    requests = (
        jnp.full((EXP_DEV, slot_count), TOK_DEV, jnp.int32)
        .at[expert_rows, slot_index]
        .set(local_ids)
    )
    requests = requests.reshape(EXP_DEV, ep_count, slot_most)
    asked_ids = lax.all_to_all(requests, "ep", split_axis=1, concat_axis=1, tiled=True)
    clipped = jnp.minimum(asked_ids, TOK_DEV - 1)
    local_expert = lax.axis_index("tp") // (tp_count // EXP_DEV)
    own_columns = lax.dynamic_slice_in_dim(
        normed, lax.axis_index("tp") * slice_width, slice_width, 1
    )
    outgoing = jnp.take(own_columns, clipped.reshape(-1), axis=0).reshape(
        EXP_DEV, ep_count, slot_most, slice_width
    )
    arrived = lax.all_to_all(outgoing, "ep", split_axis=1, concat_axis=1, tiled=True)
    copies = jnp.repeat(arrived, tp_count // EXP_DEV, axis=0)
    joined = lax.all_to_all(copies, "tp", split_axis=0, concat_axis=3, tiled=True)
    token_rows = joined.reshape(slot_count, -1)
    own_slots = lax.dynamic_index_in_dim(slot_index, local_expert, 0, keepdims=False)
    used_rows = jnp.take(token_rows, own_slots, axis=0)
    gate_weight = expert_gate.reshape(expert_gate.shape[2], expert_gate.shape[3])
    up_weight = expert_up.reshape(expert_up.shape[2], expert_up.shape[3])
    gate_values = jnp.einsum(
        "hd,rd->hr", gate_weight, used_rows, preferred_element_type=jnp.float32
    )
    up_values = jnp.einsum("hd,rd->hr", up_weight, used_rows, preferred_element_type=jnp.float32)
    part_hidden = (jax.nn.silu(gate_values) * up_values).astype(jnp.bfloat16)
    all_hidden = lax.all_gather(part_hidden, "tp", axis=0, tiled=True)
    width_hidden = expert_down.shape[1]
    placed_rows = []
    for expert_slot in range(EXP_DEV):
        hidden_block = all_hidden[expert_slot * width_hidden : (expert_slot + 1) * width_hidden, :]
        outputs = jnp.einsum(
            "fr,fd->rd", hidden_block, expert_down[expert_slot], preferred_element_type=jnp.float32
        )
        weighted = (gates[expert_slot][:, None] * outputs).astype(jnp.bfloat16)
        placed = (
            jnp.zeros((slot_count, slice_width), jnp.bfloat16)
            .at[slot_index[expert_slot]]
            .set(weighted)
        )
        placed_rows.append(placed)
    stacked = jnp.stack(placed_rows).reshape(EXP_DEV, ep_count, slot_most, slice_width)
    returned = lax.all_to_all(stacked, "ep", split_axis=1, concat_axis=1, tiled=True)
    flat_values = returned.reshape(-1, slice_width)
    flat_ids = asked_ids.reshape(-1)
    picker = (jnp.arange(TOK_DEV, dtype=jnp.int32)[:, None] == flat_ids[None, :]).astype(
        jnp.bfloat16
    )
    routed = jnp.dot(picker, flat_values, preferred_element_type=jnp.float32)
    return (shared_part + routed).astype(jnp.bfloat16)


def solution(mesh):
    return jax.shard_map(
        on_device,
        mesh=mesh,
        in_specs=(
            P("ep", "tp"),
            P(),
            P("ep", "tp"),
            P("ep", "tp"),
            P("tp", "ep"),
            P("tp", "ep", None, None),
            P("tp", "ep", None, None),
            P("ep", None, "tp"),
            P("ep", None),
            P("ep", None),
        ),
        out_specs=P("ep", "tp"),
        check_vma=False,
    )
```

profile of v0, /device:TPU:0, one launch (start us, length us, event | category | flops | bytes accessed | tf_op | source)
XLA Modules:
  0.0 314.7 jit_solution(7176182084578911614)
XLA Ops:
  6.5 0.7 all-gather.6.cloned.1.call-update
  8.7 0.7 multiply_subtract_fusion
  9.8 6.6 %gather_fusion.2 = s32[768]{0:T(1024)S(1)} fusion(s32[2,8]{1,0:T(2,128)S(1)} %sub.20, s32[768]{0:T(1024)S(1)} %reshape.205), kind=kCustom, calls=%fused_computation.2 | custom fusion | bytes 12288 | tf_op jit(solution)/shard_map/jit(take_along_axis)/gather | solution.py:58
  16.5 36.5 %scatter_fusion = s32[2,768]{1,0:T(2,128)S(1)} fusion(s32[2,768]{1,0:T(2,128)S(1)} %broadcast_in_dim.47, s32[768]{0:T(1024)S(1)} %reshape.211, s32[768]{0:T(1024)S(1)} %reshape.213), kind=kCustom, calls=%fused_computation.3 | custom fusion | bytes 15360 | tf_op jit(solution)/shard_map/scatter | solution.py:65
  53.7 5.2 %all-to-all-start = ((s32[2,8,96]{2,0,1:T(2,128)}), s32[2,8,96]{2,0,1:T(2,128)S(1)}, u32[]{:S(2)}, u32[]{:S(2)}) async-start(s32[2,8,96]{2,0,1:T(2,128)} %copy.24), calls=%async_computation.1 | async-start | bytes 16384 | tf_op jit(solution)/shard_map/all_to_all | solution.py:68
  58.9 4.9 %all-to-all-done = s32[2,8,96]{2,0,1:T(2,128)S(1)} async-done(((s32[2,8,96]{2,0,1:T(2,128)}), s32[2,8,96]{2,0,1:T(2,128)S(1)}, u32[]{:S(2)}, u32[]{:S(2)}) %all-to-all-start) | async-done | bytes 6176 | tf_op jit(solution)/shard_map/all_to_all | solution.py:68
  64.0 1.9 fusion
  66.4 1.2 copy-done.2
  67.6 5.4 %gather_fusion = bf16[1536,512]{1,0:T(8,128)(2,1)} fusion(bf16[384,512]{1,0:T(8,128)(2,1)S(1)} %constant_dynamic-slice_fusion, s32[2048]{0:T(1024)S(1)} %pad_clamp_fusion), kind=kCustom, calls=%fused_computation | custom fusion | bytes 3151872 | tf_op jit(solution)/shard_map/jit(_take)/gather | solution.py:74
  73.0 1.7 copy_select_fusion
  74.7 27.2 %all_to_all.30 = bf16[2,8,96,512]{3,2,0,1:T(8,128)(2,1)S(1)} all-to-all(bf16[2,8,96,512]{3,2,0,1:T(8,128)(2,1)S(1)} %copy_select_fusion), channel_id=1, replica_groups=mesh['tp'=4,'ep'=8] {'ep'}, dimensions={1} | all-to-all | bytes 3145728 | tf_op jit(solution)/shard_map/all_to_all | solution.py:77
  102.1 2.1 broadcast_in_dim.54
  104.2 4.9 %all-to-all-start.2 = ((bf16[4,8,96,512]{3,2,1,0:T(8,128)(2,1)}), bf16[4,8,96,512]{3,2,1,0:T(8,128)(2,1)}, u32[]{:S(2)}, u32[]{:S(2)}) async-start(bf16[4,8,96,512]{3,2,1,0:T(8,128)(2,1)} %bitcast.74), calls=%async_computation.3 | async-start | bytes 6291456 | tf_op jit(solution)/shard_map/all_to_all | solution.py:79
  109.9 68.8 %all-to-all-done.2 = bf16[4,8,96,512]{3,2,1,0:T(8,128)(2,1)} async-done(((bf16[4,8,96,512]{3,2,1,0:T(8,128)(2,1)}), bf16[4,8,96,512]{3,2,1,0:T(8,128)(2,1)}, u32[]{:S(2)}, u32[]{:S(2)}) %all-to-all-start.2) | async-done | bytes 3145760 | tf_op jit(solution)/shard_map/all_to_all | solution.py:79
  178.7 4.3 %copy.29 = bf16[1,8,96,4,512]{4,3,2,1,0:T(4,128)(2,1)S(1)} copy(bf16[1,8,96,4,512]{4,2,1,3,0:T(8,128)(2,1)} %bitcast.6) | data formatting | bytes 6291456 | tf_op jit(solution)/shard_map/all_to_all | solution.py:79
  183.1 2.7 copy.31
  185.8 7.3 %gather_fusion.1 = bf16[384,2048]{1,0:T(8,128)(2,1)} fusion(bf16[768,2048]{1,0:T(8,128)(2,1)} %bitcast.73, s32[1024]{0:T(1024)S(1)} %pad_clamp_fusion.1), kind=kCustom, calls=%fused_computation.1 | custom fusion | bytes 3147264 | tf_op jit(solution)/shard_map/jit(_take)/gather | solution.py:82
  193.1 3.3 %fusion.14 = f32[704,384]{1,0:T(8,128)S(1)} fusion(bf16[1,1,704,2048]{3,2,1,0:T(8,128)(2,1)S(1)} %copy-done, bf16[384,2048]{1,0:T(8,128)(2,1)} %gather_fusion.1, pred[384]{0:T(512)(128)(4,1)S(1)} %compare_and_fusion.1), kind=kOutput, calls=%fused_computation.26 | convolution fusion | flops 1108082688 | bytes 5538176 | tf_op jit(solution)/shard_map/hd,rd->hr/dot_general | solution.py:85
  196.5 2.6 fusion.24
  199.4 4.9 %fusion.63 = f32[384,704]{0,1:T(8,128)} fusion(bf16[384,2048]{1,0:T(8,128)(2,1)} %copy-done.2, bf16[2048,704]{0,1:T(8,128)(2,1)} %all-gather.8.cloned.1.call-done), kind=kOutput, calls=%fused_computation.87 | convolution fusion | flops 1107296256 | bytes 5537792 | tf_op jit(solution)/shard_map/dot_general | solution.py:33
  204.4 8.4 %fusion.44 = f32[384,2048]{1,0:T(8,128)} fusion(bf16[704,2048]{1,0:T(8,128)(2,1)} %all-gather.12.cloned.1.call-done, bf16[384,2048]{1,0:T(8,128)(2,1)} %copy-done.2, bf16[2048,704]{0,1:T(8,128)(2,1)} %all-gather.10.cloned.1.call-done, f32[384,704]{0,1:T(8,128)} %fusion.63), kind=kOutput, calls=%fused_computation.41 | convolution fusion | flops 2216214528 | bytes 11567104 | tf_op jit(solution)/shard_map/dot_general | solution.py:44
  213.5 29.9 %all-gather.14.cloned.1.call-done = bf16[2816,384]{1,0:T(8,128)(2,1)} async-done(((bf16[704,384]{1,0:T(8,128)(2,1)}), bf16[2816,384]{1,0:T(8,128)(2,1)}) %all-gather.14.cloned.1.call-update) | async-done | bytes 2162704 | tf_op jit(solution)/shard_map/all_gather | solution.py:90
  243.3 3.2 %fusion.35 = bf16[384,512]{1,0:T(8,128)(2,1)} fusion(bf16[2,1408,512]{2,1,0:T(8,128)(2,1)} %param.17, bf16[2816,384]{1,0:T(8,128)(2,1)} %all-gather.14.cloned.1.call-done, f32[384]{0:T(512)S(1)} %get-tuple-element.6), kind=kOutput, calls=%fused_computation.36 | convolution fusion | flops 554041344 | bytes 2917888 | tf_op jit(solution)/shard_map/fr,fd->rd/dot_general | solution.py:95
  246.6 3.3 %scatter_custom_fusion.2 = bf16[768,512]{1,0:T(8,128)(2,1)} fusion(s32[384]{0:T(512)S(1)} %get-tuple-element.9, bf16[384,512]{1,0:T(8,128)(2,1)} %fusion.35, bf16[]{:T(256)} %constant.101.clone.1), kind=kCustom, calls=%fused_computation.43 | custom fusion | bytes 786944 | tf_op jit(solution)/shard_map/scatter | solution.py:102
  249.9 3.5 %fusion.38 = bf16[384,512]{1,0:T(8,128)(2,1)} fusion(bf16[2,1408,512]{2,1,0:T(8,128)(2,1)} %param.17, bf16[2816,384]{1,0:T(8,128)(2,1)} %all-gather.14.cloned.1.call-done, f32[384]{0:T(512)S(1)} %get-tuple-element.5), kind=kOutput, calls=%fused_computation.37 | convolution fusion | flops 554041344 | bytes 2917888 | tf_op jit(solution)/shard_map/fr,fd->rd/dot_general | solution.py:95
  253.4 3.4 %scatter_custom_fusion.1 = bf16[768,512]{1,0:T(8,128)(2,1)} fusion(s32[384]{0:T(512)S(1)} %get-tuple-element.7, bf16[384,512]{1,0:T(8,128)(2,1)} %fusion.38, bf16[]{:T(256)} %constant.101.clone.1), kind=kCustom, calls=%fused_computation.45 | custom fusion | bytes 786944 | tf_op jit(solution)/shard_map/scatter | solution.py:102
  256.8 2.7 pad_maximum_fusion
  259.5 4.3 %all-to-all-start.3 = ((bf16[2,8,96,512]{3,2,0,1:T(8,128)(2,1)}), bf16[2,8,96,512]{3,2,0,1:T(8,128)(2,1)}, u32[]{:S(2)}, u32[]{:S(2)}) async-start(bf16[2,8,96,512]{3,2,0,1:T(8,128)(2,1)} %pad_maximum_fusion), calls=%async_computation.4 | async-start | bytes 3145728 | tf_op jit(solution)/shard_map/all_to_all | solution.py:106
  263.9 20.9 %all-to-all-done.3 = bf16[2,8,96,512]{3,2,0,1:T(8,128)(2,1)} async-done(((bf16[2,8,96,512]{3,2,0,1:T(8,128)(2,1)}), bf16[2,8,96,512]{3,2,0,1:T(8,128)(2,1)}, u32[]{:S(2)}, u32[]{:S(2)}) %all-to-all-start.3) | async-done | bytes 1572896 | tf_op jit(solution)/shard_map/all_to_all | solution.py:106
  284.8 2.8 copy.30
  287.6 17.2 %reduce-scatter.2.cloned.1.call-done = f32[384,512]{1,0:T(8,128)} async-done(((f32[384,2048]{1,0:T(8,128)}), f32[384,512]{1,0:T(8,128)}) %reduce-scatter.2.cloned.1.call-update) | async-done | bytes 786448 | tf_op jit(solution)/shard_map/reduce_scatter | solution.py:49
  304.7 3.1 fusion.34
  (57 shorter events, 5.2 us)
Async XLA Ops:
  6.5 186.6 %copy-start = (bf16[1,1,704,2048]{3,2,1,0:T(8,128)(2,1)S(1)}, bf16[1,1,704,2048]{3,2,1,0:T(8,128)(2,1)}, u32[]{:S(2)}) copy-start(bf16[1,1,704,2048]{3,2,1,0:T(8,128)(2,1)} %param.15) | copy-start | bytes 8650756
  6.5 57.5 %all-gather.6.cloned.1.call-start = ((), (), s32[]{:S(2)}) async-start(), calls=%async_computation.5 | async-start | bytes 1966080 | tf_op jit(solution)/shard_map/all_gather | solution.py:29
  7.3 192.1 %all-gather.8.cloned.1.call-start = ((), (), s32[]{:S(2)}) async-start(), calls=%async_computation.6 | async-start | bytes 3244032 | tf_op jit(solution)/shard_map/all_gather | solution.py:35
  8.0 196.3 %all-gather.12.cloned.1.call-start = ((), (), s32[]{:S(2)}) async-start(), calls=%async_computation.8 | async-start | bytes 3244032 | tf_op jit(solution)/shard_map/all_gather | solution.py:46
  53.0 13.0 %copy-start.4 = (f32[2048]{0:T(1024)S(1)}, f32[2048]{0:T(1024)}, u32[]{:S(2)}) copy-start(f32[2048]{0:T(1024)} %param.11) | copy-start | bytes 24580
  53.7 10.1 %all-to-all-start = ((s32[2,8,96]{2,0,1:T(2,128)}), s32[2,8,96]{2,0,1:T(2,128)S(1)}, u32[]{:S(2)}, u32[]{:S(2)}) async-start(s32[2,8,96]{2,0,1:T(2,128)} %copy.24), calls=%async_computation.1 | async-start | bytes 16384 | tf_op jit(solution)/shard_map/all_to_all | solution.py:68
  64.0 1.9 copy-start.1
  66.4 1.2 copy-start.2
  104.2 74.6 %all-to-all-start.2 = ((bf16[4,8,96,512]{3,2,1,0:T(8,128)(2,1)}), bf16[4,8,96,512]{3,2,1,0:T(8,128)(2,1)}, u32[]{:S(2)}, u32[]{:S(2)}) async-start(bf16[4,8,96,512]{3,2,1,0:T(8,128)(2,1)} %bitcast.74), calls=%async_computation.3 | async-start | bytes 6291456 | tf_op jit(solution)/shard_map/all_to_all | solution.py:79
  109.0 95.3 %all-gather.10.cloned.1.call-start = ((), (), s32[]{:S(2)}) async-start(), calls=%async_computation.7 | async-start | bytes 3244032 | tf_op jit(solution)/shard_map/all_gather | solution.py:40
  109.6 133.7 %all-gather.14.cloned.1.call-start = ((), (), s32[]{:S(2)}) async-start(), calls=%async_computation.10 | async-start | bytes 2703360 | tf_op jit(solution)/shard_map/all_gather | solution.py:90
  193.1 3.3 %copy-start.3 = (bf16[384,2048]{1,0:T(8,128)(2,1)S(1)}, bf16[384,2048]{1,0:T(8,128)(2,1)}, u32[]{:S(2)}) copy-start(bf16[384,2048]{1,0:T(8,128)(2,1)} %gather_fusion.1) | copy-start | bytes 4718596
  193.1 3.3 %copy-start.6 = (bf16[1,1,704,2048]{3,2,1,0:T(8,128)(2,1)S(1)}, bf16[1,1,704,2048]{3,2,1,0:T(8,128)(2,1)}, u32[]{:S(2)}) copy-start(bf16[1,1,704,2048]{3,2,1,0:T(8,128)(2,1)} %param.16) | copy-start | bytes 8650756
  199.1 105.6 %reduce-scatter.2.cloned.1.call-start = ((), (), s32[]{:S(2)}) async-start(), calls=%async_computation.9 | async-start | bytes 3932160 | tf_op jit(solution)/shard_map/reduce_scatter | solution.py:49
  212.8 0.7 copy-start.5
  259.5 25.3 %all-to-all-start.3 = ((bf16[2,8,96,512]{3,2,0,1:T(8,128)(2,1)}), bf16[2,8,96,512]{3,2,0,1:T(8,128)(2,1)}, u32[]{:S(2)}, u32[]{:S(2)}) async-start(bf16[2,8,96,512]{3,2,0,1:T(8,128)(2,1)} %pad_maximum_fusion), calls=%async_computation.4 | async-start | bytes 3145728 | tf_op jit(solution)/shard_map/all_to_all | solution.py:106
Sparse Core Ops, SparseCore 0:
  8.9 39.7 all-gather.5
  50.6 30.5 all-gather.7
  83.0 35.6 all-gather.11
  120.5 31.5 all-gather.9
  199.2 44.0 all-gather.13
  245.5 59.1 reduce-scatter.1
where the time goes:
time: 315 us
  waiting for transfers between devices  144 us (46%)
  local copies, waits for them, and re-layouts  77.4 us (25%)
  matrix products  29.2 us (9%)
  blocking collectives  27.2 us (9%)
  starting transfers between devices  15 us (5%)
  between operations  13.7 us (4%)
  other arithmetic  7.88 us (3%)
    all_to_all x1, waiting for transfers between devices, on_device(): lax.all_to_all(copies, 'tp', split_axis=0, concat_axis=3, tiled=True)  68.8 us
    scatter x1, local copies, waits for them, and re-layouts, on_device(): requests = jnp.full((EXP_DEV, slot_count), TOK_DEV, jnp.int32).at[expert_...  36.5 us
    all_gather x1, waiting for transfers between devices, on_device(): all_hidden = lax.all_gather(part_hidden, 'tp', axis=0, tiled=True)  29.9 us
    all_to_all x1, blocking collectives, on_device(): lax.all_to_all(outgoing, 'ep', split_axis=1, concat_axis=1, tiled=True)  27.2 us
    all_to_all x1, waiting for transfers between devices, on_device(): lax.all_to_all(stacked, 'ep', split_axis=1, concat_axis=1, tiled=True)  20.9 us
    reduce_scatter x1, waiting for transfers between devices, on_device(): lax.psum_scatter(partial_out, 'tp', scatter_dimension=1, tiled=True)  17.2 us
    dot_general x1, matrix products, on_device(): jnp.dot(shared_hidden, lax.all_gather(shared_down, 'ep', axis=1, tiled=Tr...  8.41 us
    gather x1, local copies, waits for them, and re-layouts, on_device(): used_rows = jnp.take(token_rows, own_slots, axis=0)  7.34 us
  transfers between devices with their start and end apart: 9, of which 5 were waited for; matrix products, arithmetic and copies ran while one was open for 35% of the time, Pallas kernels for 0%

commit v1 on v0

v1 whole, which is shorter than its diff:
```python
import functools

import jax
import jax.numpy as jnp
from jax import lax
from jax.experimental import pallas as pl
from jax.experimental.pallas import tpu as pltpu
from jax.sharding import PartitionSpec as P

norm_eps = 1e-06
MESH = pl.DeviceIdType.MESH


def flip(index, mask):
    bit = 1
    result = index
    while bit <= mask:
        if mask & bit:
            result = result + bit - 2 * bit * ((index // bit) % 2)
        bit *= 2
    return result


def bits_below(count):
    return [1 << i for i in range(count.bit_length() - 1)]


def half_orders(count):
    bits = bits_below(count)
    upper = bits[1:]
    return [upper + bits[:1], upper[::-1] + bits[:1]]


def later_hops(mask, order):
    last = max([i for i, b in enumerate(order) if mask & b], default=-1)
    return order[last + 1 :]


def masks_by_level(count):
    return sorted(range(1, count), key=lambda m: (bin(m).count("1"), -m))


def levels(count):
    found = {}
    for m in masks_by_level(count):
        found.setdefault(bin(m).count("1"), []).append(m)
    return [found[k] for k in sorted(found)]


def gather_kernel(
    n_tp,
    n_ep,
    tok_ref,
    sg_ref,
    su_ref,
    sd_ref,
    chosen_ref,
    sg_out,
    su_out,
    sd_out,
    own_out,
    used_out,
    tok_all,
    sel,
    total,
    ep_send,
    ep_recv,
    tp_send,
    tp_recv,
    disp_send,
    disp_recv,
    local_sem,
):
    tp = lax.axis_index("tp")
    ep = lax.axis_index("ep")
    n_exp, cap = chosen_ref.shape[0], chosen_ref.shape[1]
    n_tok, width = tok_ref.shape
    split = n_tp // n_exp
    slot = tp // split
    orders = half_orders(n_ep)
    high_masks = [k * split for k in range(1, n_exp)]
    tp_bits = bits_below(n_tp)
    tp_order = tp_bits[::-1]
    tp_partners = sorted(set(tp_bits) | set(high_masks))

    barrier = pltpu.get_barrier_semaphore()
    for b in bits_below(n_ep):
        pl.semaphore_signal(barrier, inc=1, device_id={"ep": flip(ep, b)}, device_id_type=MESH)
    for b in tp_partners:
        pl.semaphore_signal(barrier, inc=1, device_id={"tp": flip(tp, b)}, device_id_type=MESH)
    pl.semaphore_wait(barrier, len(bits_below(n_ep)) + len(tp_partners))

    def block_of(out, block, rows):
        if len(out.shape) == 3:
            return out.at[block, rows, :]
        cols = out.shape[1] // n_ep
        return out.at[rows, pl.ds(pl.multiple_of(block * cols, cols), cols)]

    def sources(w):
        return [tok_ref, sg_ref, su_ref, sd_ref][w]

    def own_piece(w, h):
        ref = sources(w)
        half = ref.shape[0] // 2
        return ref.at[pl.ds(h * half, half), :]

    def piece(w, block, h):
        ref = sources(w)
        half = ref.shape[0] // 2
        if w == 0:
            return tok_all.at[block, pl.ds(h * half, half), :]
        return block_of([None, sg_out, su_out, sd_out][w], block, pl.ds(h * half, half))

    def ep_copy(w, h, mask, hop):
        return pltpu.make_async_remote_copy(
            src_ref=own_piece(w, h) if mask == 0 else piece(w, flip(ep, mask), h),
            dst_ref=piece(w, flip(ep, mask), h),
            send_sem=ep_send.at[w, h, mask | hop],
            recv_sem=ep_recv.at[w, h, mask | hop],
            device_id={"ep": flip(ep, hop)},
            device_id_type=MESH,
        )

    def ep_arrival(w, h, mask):
        order = orders[h]
        hop = [b for b in order if mask & b][-1]
        dst = piece(w, flip(ep, mask), h)
        return pltpu.make_async_remote_copy(
            src_ref=dst,
            dst_ref=dst,
            send_sem=ep_send.at[w, h, mask],
            recv_sem=ep_recv.at[w, h, mask],
            device_id={"ep": flip(ep, hop)},
            device_id_type=MESH,
        )

    def ep_start(w):
        for position in range(len(orders[0])):
            for h in (0, 1):
                ep_copy(w, h, 0, orders[h][position]).start()

    def ep_level(w, masks):
        for mask in masks:
            for h in (0, 1):
                ep_arrival(w, h, mask).wait_recv()
                for hop in later_hops(mask, orders[h]):
                    ep_copy(w, h, mask, hop).start()

    def columns(ref, block):
        return ref.at[:, pl.ds(pl.multiple_of(block * width, width), width)]

    def tp_copy(mask, hop):
        return pltpu.make_async_remote_copy(
            src_ref=tok_ref if mask == 0 else columns(own_out, flip(tp, mask)),
            dst_ref=columns(own_out, flip(tp, mask)),
            send_sem=tp_send.at[mask | hop],
            recv_sem=tp_recv.at[mask | hop],
            device_id={"tp": flip(tp, hop)},
            device_id_type=MESH,
        )

    def disp_copy(mask, hop):
        if mask == 0:
            src = sel.at[flip(tp, hop) // split]
        else:
            src = columns(used_out, flip(tp, mask))
        return pltpu.make_async_remote_copy(
            src_ref=src,
            dst_ref=columns(used_out, flip(tp, mask)),
            send_sem=disp_send.at[mask | hop],
            recv_sem=disp_recv.at[mask | hop],
            device_id={"tp": flip(tp, hop)},
            device_id_type=MESH,
        )

    def low_hops(mask):
        low = mask % split
        return [b for b in bits_below(split) if b > low]

    def local_copies():
        items = [(0, tok_ref, tok_all.at[ep]), (1, tok_ref, columns(own_out, tp))]
        pairs = ((sg_ref, sg_out), (su_ref, su_out), (sd_ref, sd_out))
        for i, (ref, out) in enumerate(pairs):
            items.append((2 + i, ref, block_of(out, ep, pl.ds(0, ref.shape[0]))))
        return [pltpu.make_async_copy(s, d, local_sem.at[i]) for i, s, d in items]

    ep_start(0)
    tp_copy(0, tp_order[0]).start()
    locals_started = local_copies()
    for copy in locals_started:
        copy.start()
    ep_levels = levels(n_ep)
    ep_level(0, ep_levels[0])
    for w in (1, 2, 3):
        ep_start(w)
    for masks in ep_levels[1:]:
        ep_level(0, masks)
    locals_started[0].wait()

    for s in range(n_exp):
        total[...] = jnp.zeros_like(total)

        def add_source(e, carry):
            ids = lax.broadcasted_iota(jnp.int32, (cap, n_tok), 1) + e * n_tok
            hits = jnp.where(chosen_ref[s] == ids, 1.0, 0.0).astype(jnp.bfloat16)
            total[...] += jnp.dot(hits, tok_all[e], preferred_element_type=jnp.float32)
            return carry

        lax.fori_loop(0, n_ep, add_source, 0)
        sel[s] = total[...].astype(jnp.bfloat16)

    for mask in high_masks:
        disp_copy(0, mask).start()
    for hop in low_hops(0):
        disp_copy(0, hop).start()
    own_used = pltpu.make_async_copy(sel.at[slot], columns(used_out, tp), local_sem.at[5])
    own_used.start()

    for w in (1, 2, 3):
        ep_level(w, ep_levels[0])
    for mask in high_masks:
        disp_wait(
            columns(used_out, flip(tp, mask)), disp_send, disp_recv, mask, tp
        )
        for hop in low_hops(mask):
            disp_copy(mask, hop).start()
    for hop in tp_order[1:]:
        tp_copy(0, hop).start()
    tp_seen = []
    for mask in sorted(range(1, n_tp), key=lambda m: [tp_order.index(b) for b in tp_order if m & b][-1]):
        last = [b for b in tp_order if mask & b][-1]
        if last == tp_order[0]:
            disp_wait(columns(own_out, flip(tp, mask)), tp_send, tp_recv, mask, tp)
            tp_seen.append(mask)
            for hop in later_hops(mask, tp_order):
                tp_copy(mask, hop).start()
    for masks in ep_levels[1:]:
        for w in (1, 2, 3):
            ep_level(w, masks)
    for mask in range(1, n_tp):
        if mask not in high_masks:
            disp_wait(columns(used_out, flip(tp, mask)), disp_send, disp_recv, mask, tp)
            for hop in low_hops(mask):
                disp_copy(mask, hop).start()
    for mask in sorted(range(1, n_tp), key=lambda m: [tp_order.index(b) for b in tp_order if m & b][-1]):
        if mask not in tp_seen:
            disp_wait(columns(own_out, flip(tp, mask)), tp_send, tp_recv, mask, tp)
            for hop in later_hops(mask, tp_order):
                tp_copy(mask, hop).start()

    for copy in locals_started[1:]:
        copy.wait()
    own_used.wait()
    for w in range(4):
        for h in (0, 1):
            for mask in range(n_ep):
                for hop in later_hops(mask, orders[h]):
                    ep_copy(w, h, mask, hop).wait_send()
    for mask in range(n_tp):
        for hop in later_hops(mask, tp_order):
            tp_copy(mask, hop).wait_send()
    for mask in [0] + high_masks + [m for m in range(1, n_tp) if m not in high_masks]:
        hops = low_hops(mask)
        if mask == 0:
            hops = high_masks + hops
        for hop in hops:
            disp_copy(mask, hop).wait_send()


def disp_wait(dst, send_sem, recv_sem, mask, tp):
    pltpu.make_async_remote_copy(
        src_ref=dst,
        dst_ref=dst,
        send_sem=send_sem.at[mask],
        recv_sem=recv_sem.at[mask],
        device_id={"tp": flip(tp, mask)},
        device_id_type=MESH,
    ).wait_recv()


def upfront(n_tp, n_ep, tokens, shared_gate, shared_up, shared_down, chosen):
    n_tok, width = tokens.shape
    n_exp, cap = chosen.shape
    vmem = pl.BlockSpec(memory_space=pltpu.VMEM)
    hbm = pl.BlockSpec(memory_space=pl.ANY)
    bf16 = jnp.bfloat16

    def joined(weight):
        rows, cols = weight.shape
        if cols % 128 == 0:
            return jax.ShapeDtypeStruct((rows, n_ep * cols), bf16)
        return jax.ShapeDtypeStruct((n_ep, rows, cols), bf16)

    return pl.pallas_call(
        functools.partial(gather_kernel, n_tp, n_ep),
        out_shape=(
            joined(shared_gate),
            joined(shared_up),
            joined(shared_down),
            jax.ShapeDtypeStruct((n_tok, n_tp * width), bf16),
            jax.ShapeDtypeStruct((cap, n_tp * width), bf16),
        ),
        in_specs=[vmem] * 5,
        out_specs=(hbm,) * 5,
        scratch_shapes=[
            pltpu.VMEM((n_ep, n_tok, width), bf16),
            pltpu.VMEM((n_exp, cap, width), bf16),
            pltpu.VMEM((cap, width), jnp.float32),
            pltpu.SemaphoreType.DMA((4, 2, n_ep)),
            pltpu.SemaphoreType.DMA((4, 2, n_ep)),
            pltpu.SemaphoreType.DMA((n_tp,)),
            pltpu.SemaphoreType.DMA((n_tp,)),
            pltpu.SemaphoreType.DMA((n_tp,)),
            pltpu.SemaphoreType.DMA((n_tp,)),
            pltpu.SemaphoreType.DMA((6,)),
        ],
        compiler_params=pltpu.CompilerParams(
            collective_id=0, has_side_effects=True, vmem_limit_bytes=48 * 1024 * 1024
        ),
    )(tokens, shared_gate, shared_up, shared_down, chosen[:, :, None])


def flat_weight(weight):
    if weight.ndim == 2:
        return weight
    return jnp.moveaxis(weight, 0, 1).reshape(weight.shape[1], -1)


def normalise(rows, gain):
    widened = rows.astype(jnp.float32)
    inv_scale = lax.rsqrt(jnp.mean(widened * widened, axis=1, keepdims=True) + norm_eps)
    return (widened * inv_scale * gain).astype(jnp.bfloat16)


def swap_tp(value, n_tp, mask):
    return lax.ppermute(value, "tp", [(i, i ^ mask) for i in range(n_tp)])


def gather_tp(block, n_tp):
    tp = lax.axis_index("tp")
    held = block[None]
    for bit in bits_below(n_tp)[::-1]:
        other = swap_tp(held, n_tp, bit)
        upper = (tp // bit) % 2 == 1
        first = jnp.where(upper, other, held)
        second = jnp.where(upper, held, other)
        held = jnp.stack([first, second], axis=1).reshape((-1,) + block.shape)
    return held


def scatter_sum_tp(partial, n_tp):
    tp = lax.axis_index("tp")
    rows = partial.shape[0]
    width = partial.shape[1] // n_tp
    blocks = [partial[:, i * width : (i + 1) * width] for i in range(n_tp)]
    for bit in bits_below(n_tp):
        upper = (tp // bit) % 2 == 1
        send = [jnp.where(upper, blocks[i], blocks[i + 1]) for i in range(0, len(blocks), 2)]
        keep = [jnp.where(upper, blocks[i + 1], blocks[i]) for i in range(0, len(blocks), 2)]
        got = swap_tp(jnp.stack(send).astype(jnp.bfloat16), n_tp, bit)
        blocks = [k + got[i].astype(jnp.float32) for i, k in enumerate(keep)]
    return blocks[0]


def on_device(
    tokens,
    norm_gain,
    shared_gate,
    shared_up,
    shared_down,
    expert_gate,
    expert_up,
    expert_down,
    chosen,
    gates,
):
    n_tp = lax.axis_size("tp")
    n_ep = lax.axis_size("ep")
    ep = lax.axis_index("ep")
    n_exp, cap = chosen.shape
    n_tok, width = tokens.shape
    f32 = jnp.float32

    all_chosen = lax.all_gather(chosen, "ep", axis=0, tiled=True)
    sg, su, sd, own_rows, used_rows = upfront(
        n_tp, n_ep, tokens, shared_gate.T, shared_up.T, shared_down, chosen
    )
    sg, su, sd = flat_weight(sg), flat_weight(su), flat_weight(sd)

    slot_most = 2 * cap // n_ep
    positions = jnp.arange(cap, dtype=jnp.int32)
    sources = chosen // n_tok
    before = chosen[:, None, :] < (sources * n_tok)[:, :, None]
    run_start = jnp.sum(before.astype(jnp.int32), axis=2)
    slot_index = sources * slot_most + positions[None, :] - run_start
    first = jnp.sum((all_chosen < ep * n_tok).astype(jnp.int32), axis=1)
    stop = jnp.sum((all_chosen < (ep + 1) * n_tok).astype(jnp.int32), axis=1)
    slots = jnp.arange(slot_most, dtype=jnp.int32)
    wanted = first[:, None] + slots[None, :]
    wanted = jnp.where(wanted < stop[:, None], wanted, -1)
    own_ids = jnp.sum(
        jnp.where(
            wanted[:, :, None] == positions[None, None, :],
            (all_chosen - ep * n_tok + 1)[:, None, :],
            0,
        ),
        axis=2,
    ) - 1

    used = normalise(used_rows, norm_gain)
    gate_weight = expert_gate.reshape(expert_gate.shape[2], expert_gate.shape[3])
    up_weight = expert_up.reshape(expert_up.shape[2], expert_up.shape[3])
    gate_values = jnp.einsum("hd,rd->hr", gate_weight, used, preferred_element_type=f32)
    up_values = jnp.einsum("hd,rd->hr", up_weight, used, preferred_element_type=f32)
    part_hidden = (jax.nn.silu(gate_values) * up_values).astype(jnp.bfloat16)
    all_hidden = gather_tp(part_hidden, n_tp)

    normed = normalise(own_rows, norm_gain)
    gate_sum = jnp.einsum("rd,hd->rh", normed, sg, preferred_element_type=f32)
    up_sum = jnp.einsum("rd,hd->rh", normed, su, preferred_element_type=f32)
    shared_hidden = (jax.nn.silu(gate_sum) * up_sum).astype(jnp.bfloat16)
    partial_out = jnp.dot(shared_hidden, sd, preferred_element_type=f32)
    shared_part = scatter_sum_tp(partial_out, n_tp)

    hidden = all_hidden.reshape(n_exp, expert_down.shape[1], cap)
    placed = []
    for s in range(n_exp):
        outputs = jnp.einsum("fr,fd->rd", hidden[s], expert_down[s], preferred_element_type=f32)
        weighted = (gates[s][:, None] * outputs).astype(jnp.bfloat16)
        placer = jnp.arange(n_ep * slot_most, dtype=jnp.int32)[:, None] == slot_index[s][None, :]
        placed.append(
            jnp.dot(placer.astype(jnp.bfloat16), weighted, preferred_element_type=f32)
            .astype(jnp.bfloat16)
            .reshape(n_ep, slot_most, width)
        )
    stacked = jnp.concatenate(placed, axis=1)
    returned = lax.all_to_all(stacked, "ep", split_axis=0, concat_axis=0, tiled=True)
    flat_values = returned.reshape(-1, width)
    flat_ids = own_ids.reshape(-1)
    picker = jnp.arange(n_tok, dtype=jnp.int32)[:, None] == flat_ids[None, :]
    routed = jnp.dot(picker.astype(jnp.bfloat16), flat_values, preferred_element_type=f32)
    return (shared_part + routed).astype(jnp.bfloat16)


def solution(mesh):
    return jax.shard_map(
        on_device,
        mesh=mesh,
        in_specs=(
            P("ep", "tp"),
            P(),
            P("ep", "tp"),
            P("ep", "tp"),
            P("tp", "ep"),
            P("tp", "ep", None, None),
            P("tp", "ep", None, None),
            P("ep", None, "tp"),
            P("ep", None),
            P("ep", None),
        ),
        out_specs=P("ep", "tp"),
        check_vma=False,
    )
```

time: 315 us -> 211 us (0.67)
  waiting for transfers between devices: 144 us -> 49.4 us
  Pallas kernels: 0 us -> 75.3 us
  local copies, waits for them, and re-layouts: 77.4 us -> 6.25 us
  between operations: 13.7 us -> 0.23 us
  other arithmetic: 7.88 us -> 21 us
  starting transfers between devices: 15 us -> 8.7 us
  blocking collectives: 27.2 us -> 21.9 us
    all_to_all x3 -> x1, waiting for transfers between devices: 94.6 us -> 0.01 us  [on_device(): lax.all_to_all(stacked, 'ep', split_axis=0, concat_axis=0, tiled=True)]
    pallas_call x0 -> x1, Pallas kernels: none -> 75.3 us  [upfront(): pl.pallas_call(functools.partial(gather_kernel, n_tp, n_ep), out_shape=(j...]
    ppermute x0 -> x4, waiting for transfers between devices: none -> 49.4 us  [swap_tp(): return lax.ppermute(value, 'tp', [(i, i ^ mask) for i in range(n_tp)])]
    scatter x3 -> x0, local copies, waits for them, and re-layouts: 43.2 us -> none  [the longest x1 36.5 us: on_device(): requests = jnp.full((EXP_DEV, slot_count), TOK_DEV, jnp.int32).at[expert_...]
    all_gather x5 -> x0, waiting for transfers between devices: 29.9 us -> none  [the longest x1 29.9 us: on_device(): all_hidden = lax.all_gather(part_hidden, 'tp', axis=0, tiled=True)]
    all_to_all x1 -> x0, blocking collectives: 27.2 us -> none  [on_device(): lax.all_to_all(outgoing, 'ep', split_axis=1, concat_axis=1, tiled=True)]
    all_gather x0 -> x1, blocking collectives: none -> 21.9 us  [on_device(): all_chosen = lax.all_gather(chosen, 'ep', axis=0, tiled=True)]
    gather x5 -> x0, local copies, waits for them, and re-layouts: 19.4 us -> none  [the longest x1 7.34 us: on_device(): used_rows = jnp.take(token_rows, own_slots, axis=0)]
  transfers between devices with their start and end apart: 9 -> 5, of which waited for: 5 -> 3; matrix products, arithmetic and copies ran while one was open for 35% -> 12% of each run, Pallas kernels for 0% -> 0%
where the time goes in v1:
time: 211 us; the launch traced here: 210 us
  Pallas kernels  75.3 us (36%)
  waiting for transfers between devices  49.4 us (23%)
  matrix products  27.1 us (13%)
  blocking collectives  21.9 us (10%)
  other arithmetic  21 us (10%)
  starting transfers between devices  8.7 us (4%)
  local copies, waits for them, and re-layouts  6.25 us (3%)
    pallas_call x1, Pallas kernels, upfront(): pl.pallas_call(functools.partial(gather_kernel, n_tp, n_ep), out_shape=(j...  75.3 us
    ppermute x4, waiting for transfers between devices, swap_tp(): return lax.ppermute(value, 'tp', [(i, i ^ mask) for i in range(n_tp)])  49.4 us
    all_gather x1, blocking collectives, on_device(): all_chosen = lax.all_gather(chosen, 'ep', axis=0, tiled=True)  21.9 us
    dot_general x1, matrix products, on_device(): partial_out = jnp.dot(shared_hidden, sd, preferred_element_type=f32)  8.23 us
    dot_general x2, matrix products, on_device(): jnp.dot(placer.astype(jnp.bfloat16), weighted, preferred_element_type=f32)  7.85 us
    dot_general x1, matrix products, on_device(): gate_sum = jnp.einsum('rd,hd->rh', normed, sg, preferred_element_type=f32)  5.03 us
    unnamed x30, local copies, waits for them, and re-layouts  4.94 us
    another operation x2, other arithmetic, scatter_sum_tp(): got = swap_tp(jnp.stack(send).astype(jnp.bfloat16), n_tp, bit)  4.88 us
  transfers between devices with their start and end apart: 5, of which 3 were waited for; matrix products, arithmetic and copies ran while one was open for 12% of the time, Pallas kernels for 0%

profile of v1, /device:TPU:0, one launch (start us, length us, event | category | flops | bytes accessed | tf_op | source)
XLA Modules:
  0.0 209.9 jit_solution(1310837594314387782)
XLA Ops:
  0.0 1.0 copy.13.chosen_ref
  1.0 1.0 copy-done.2
  2.0 1.0 copy-done.3
  3.0 1.0 copy-done.4
  4.0 1.0 copy-done.5
  5.0 75.3 %shard_map.100 = (bf16[704,2048]{1,0:T(8,128)(2,1)}, bf16[704,2048]{1,0:T(8,128)(2,1)}, bf16[704,2048]{1,0:T(8,128)(2,1)}, bf16[384,2048]{1,0:T(8,128)(2,1)S(1)}, bf16[384,2048]{1,0:T(8,128)(2,1)S(1)}) custom-call(bf16[384,512]{1,0:T(8,128)(2,1)S(1)} %copy-done.2, bf16[704,256]{1,0:T(8,128)(2,1)S(1)} %bitcast.102, bf16[704,256]{1,0:T(8,128)(2,1)S(1)} %bitcast.103, ...), custom_call_target="tpu_custom_call" | custom-call | tf_op jit(solution)/shard_map/pallas_call | solution.py:294
  80.3 0.4 fusion.3
  80.8 1.8 fusion.17
  82.7 1.9 fusion.42
  84.6 3.6 %collective-permute-start.2 = (bf16[1,704,384]{2,1,0:T(8,128)(2,1)S(1)}, bf16[1,704,384]{2,1,0:T(8,128)(2,1)}, u32[]{:S(2)}, u32[]{:S(2)}) collective-permute-start(bf16[1,704,384]{2,1,0:T(8,128)(2,1)S(1)} %fusion.42), channel_id=1, source_target_pairs={{0,16},{8,24},{16,0},{24,8},{1,17},{9,25},{17,1},{25,9},{2,18},{10... | collective-permute-start | bytes 1622024 | tf_op jit(solution)/shard_map/ppermute | solution.py:336
  88.2 0.4 fusion
  89.0 5.0 %fusion.61 = f32[384,704]{0,1:T(8,128)} fusion(bf16[704,2048]{1,0:T(8,128)(2,1)} %get-tuple-element.11, bf16[384,2048]{1,0:T(8,128)(2,1)} %copy-done.1, f32[2048]{0:T(1024)S(1)} %copy-done.14, f32[384]{0:T(512)S(1)} %add_rsqrt_fusion.1), kind=kOutput, calls=%fused_computation.64 | convolution fusion | flops 1110441984 | bytes 5547520 | tf_op jit(solution)/shard_map/rd,hd->rh/dot_general | solution.py:419
  94.0 17.8 %collective-permute-done.2 = bf16[1,704,384]{2,1,0:T(8,128)(2,1)} collective-permute-done((bf16[1,704,384]{2,1,0:T(8,128)(2,1)S(1)}, bf16[1,704,384]{2,1,0:T(8,128)(2,1)}, u32[]{:S(2)}, u32[]{:S(2)}) %collective-permute-start.2) | collective-permute-done | bytes 540704 | tf_op jit(solution)/shard_map/ppermute | solution.py:336
  111.8 1.3 select_bitcast_fusion.3
  113.1 0.8 copy-done.7
  113.9 1.2 maximum_bitcast_fusion
  115.1 8.2 %fusion.53 = f32[384,2048]{1,0:T(8,128)} fusion(bf16[704,2048]{1,0:T(8,128)(2,1)} %get-tuple-element.13, bf16[704,2048]{1,0:T(8,128)(2,1)} %get-tuple-element.12, f32[384,704]{0,1:T(8,128)} %fusion.61, bf16[384,2048]{1,0:T(8,128)(2,1)} %copy-done.1, f32[2048]{0:T(1024)S(1)} %copy-done.14, f32[384]{0:T(512)S(1)} %add_rsqrt_fusion.1), kind=kOutput, calls=%fused_computation.58 | convolution fusion | flops 2219360256 | bytes 11576832 | tf_op jit(solution)/shard_map/dot_general | solution.py:422
  123.4 2.9 %fusion.63 = (bf16[1,384,512]{2,1,0:T(8,128)(2,1)}, bf16[1,384,512]{2,1,0:T(8,128)(2,1)}) fusion(f32[384,2048]{1,0:T(8,128)} %fusion.53, pred[]{:T(512)S(6)} %eq.70), kind=kLoop, calls=%fused_computation.65 | loop fusion | flops 393216 | bytes 2359297 | tf_op jit(solution)/shard_map/stack | solution.py:360
  126.3 13.8 %collective-permute-done.3 = bf16[2,704,384]{2,1,0:T(8,128)(2,1)} collective-permute-done((bf16[2,704,384]{2,1,0:T(8,128)(2,1)}, bf16[2,704,384]{2,1,0:T(8,128)(2,1)}, u32[]{:S(2)}, u32[]{:S(2)}) %collective-permute-start.3) | collective-permute-done | bytes 1081376 | tf_op jit(solution)/shard_map/ppermute | solution.py:336
  140.1 1.5 select_bitcast_fusion.1
  141.6 1.6 fusion.50
  143.2 3.9 %convolution_convert_fusion.1 = bf16[768,512]{1,0:T(8,128)(2,1)} fusion(bf16[1408,384]{1,0:T(8,128)(2,1)} %bitcast.105, bf16[2,1408,512]{2,1,0:T(8,128)(2,1)} %param.17, s32[384]{0:T(512)S(1)} %get-tuple-element.19, f32[384]{0:T(512)S(1)} %get-tuple-element.17), kind=kOutput, calls=%fused_computation.28 | convolution fusion | flops 856719360 | bytes 3312640 | tf_op jit(solution)/shard_map/dot_general | solution.py:432
  147.1 3.9 %convolution_convert_fusion = bf16[768,512]{1,0:T(8,128)(2,1)} fusion(bf16[1408,384]{1,0:T(8,128)(2,1)} %bitcast.104, bf16[2,1408,512]{2,1,0:T(8,128)(2,1)} %param.17, s32[384]{0:T(512)S(1)} %get-tuple-element.20, f32[384]{0:T(512)S(1)} %get-tuple-element.18), kind=kOutput, calls=%fused_computation.27 | convolution fusion | flops 856719360 | bytes 3312640 | tf_op jit(solution)/shard_map/dot_general | solution.py:432
  151.1 2.6 %pad_maximum_fusion = bf16[8,192,512]{2,1,0:T(8,128)(2,1)} fusion(bf16[8,96,512]{2,1,0:T(8,128)(2,1)} %bitcast.107, bf16[8,96,512]{2,1,0:T(8,128)(2,1)} %bitcast.106), kind=kLoop, calls=%fused_computation.20 | loop fusion | flops 3145728 | bytes 3145728 | tf_op jit(solution)/shard_map/concatenate | solution.py:436
  153.7 4.4 %all-to-all-start = ((bf16[8,192,512]{2,1,0:T(8,128)(2,1)}), bf16[8,192,512]{2,1,0:T(8,128)(2,1)}, u32[]{:S(2)}, u32[]{:S(2)}) async-start(bf16[8,192,512]{2,1,0:T(8,128)(2,1)} %pad_maximum_fusion), calls=%async_computation | async-start | bytes 3145728 | tf_op jit(solution)/shard_map/all_to_all | solution.py:437
  158.1 1.9 pad_maximum_fusion.2
  160.4 21.9 %all-gather = s32[8,2,384]{2,1,0:T(2,128)S(1)} all-gather(s32[1,2,384]{2,1,0:T(2,128)S(1)} %bitcast.109), channel_id=1, replica_groups=mesh['tp'=4,'ep'=8] {'ep'}, dimensions={0}, use_global_device_ids=true | all-gather | bytes 27648 | tf_op jit(solution)/shard_map/all_gather | solution.py:384
  182.9 0.7 select_reduce_fusion
  183.6 3.3 %fusion.65 = bf16[1,384,512]{2,1,0:T(8,128)(2,1)} fusion(pred[]{:T(512)S(6)} %eq.69, bf16[2,384,512]{2,1,0:T(8,128)(2,1)} %collective-permute-done, f32[384,2048]{1,0:T(8,128)} %fusion.53, pred[]{:T(512)S(6)} %eq.70), kind=kLoop, calls=%fused_computation.67 | loop fusion | flops 1572864 | bytes 4325378 | tf_op jit(solution)/shard_map/convert_element_type | solution.py:360
  187.3 2.3 %fusion.10 = f32[384,512]{1,0:T(8,128)S(1)} fusion(bf16[1536,512]{1,0:T(8,128)(2,1)} %bitcast.26, s32[1536]{0:T(1024)S(1)} %sub.29), kind=kOutput, calls=%fused_computation.17 | convolution fusion | flops 604569600 | bytes 2365440 | tf_op jit(solution)/shard_map/dot_general | solution.py:441
  189.6 17.8 %collective-permute-done.1 = bf16[1,384,512]{2,1,0:T(8,128)(2,1)S(1)} collective-permute-done((bf16[1,384,512]{2,1,0:T(8,128)(2,1)}, bf16[1,384,512]{2,1,0:T(8,128)(2,1)S(1)}, u32[]{:S(2)}, u32[]{:S(2)}) %collective-permute-start.1) | collective-permute-done | bytes 393248 | tf_op jit(solution)/shard_map/ppermute | solution.py:336
  207.5 2.4 %fusion.52 = bf16[384,512]{1,0:T(8,128)(2,1)} fusion(f32[384,512]{1,0:T(8,128)S(1)} %fusion.10, bf16[1,384,512]{2,1,0:T(8,128)(2,1)S(1)} %collective-permute-done.1, pred[]{:T(512)S(6)} %eq.69, bf16[2,384,512]{2,1,0:T(8,128)(2,1)} %collective-permute-done, f32[384,2048]{1,0:T(8,128)S(1)} %copy-done.6, pred[]{:T(512)S(6)} %eq.70), kind=kLoop, calls=%fused_computation.52 | loop fusion | flops 2162688 | bytes 5505026 | tf_op jit(solution)/shard_map/convert_element_type | solution.py:442
  (44 shorter events, 1.9 us)
Async XLA Ops:
  0.0 80.7 %copy-start = (bf16[1,1,704,2048]{3,2,1,0:T(8,128)(2,1)S(1)}, bf16[1,1,704,2048]{3,2,1,0:T(8,128)(2,1)}, u32[]{:S(2)}) copy-start(bf16[1,1,704,2048]{3,2,1,0:T(8,128)(2,1)} %param.15) | copy-start | bytes 8650756
  1.0 1.0 copy-start.2
  2.0 1.0 copy-start.3
  3.0 1.0 copy-start.4
  4.0 1.0 copy-start.5
  5.0 75.8 %copy-start.14 = (f32[2048]{0:T(1024)S(1)}, f32[2048]{0:T(1024)}, u32[]{:S(2)}) copy-start(f32[2048]{0:T(1024)} %param.11) | copy-start | bytes 24580
  80.3 7.9 %copy-start.1 = (bf16[384,2048]{1,0:T(8,128)(2,1)}, bf16[384,2048]{1,0:T(8,128)(2,1)S(1)}, u32[]{:S(2)}) copy-start(bf16[384,2048]{1,0:T(8,128)(2,1)S(1)} %get-tuple-element.10) | copy-start | bytes 4718596
  80.7 1.9 copy-start.13
  82.7 5.5 %copy-start.11 = (s32[2,384]{1,0:T(2,128)S(1)}, s32[2,384]{1,0:T(2,128)}, u32[]{:S(2)}) copy-start(s32[2,384]{1,0:T(2,128)} %param.18) | copy-start | bytes 9220
  84.5 9.5 %copy-start.10 = (bf16[1,704,384]{2,1,0:T(8,128)(2,1)}, bf16[1,704,384]{2,1,0:T(8,128)(2,1)S(1)}, u32[]{:S(2)}) copy-start(bf16[1,704,384]{2,1,0:T(8,128)(2,1)S(1)} %fusion.42) | copy-start | bytes 1622020
  84.6 27.2 %collective-permute-start.2 = (bf16[1,704,384]{2,1,0:T(8,128)(2,1)S(1)}, bf16[1,704,384]{2,1,0:T(8,128)(2,1)}, u32[]{:S(2)}, u32[]{:S(2)}) collective-permute-start(bf16[1,704,384]{2,1,0:T(8,128)(2,1)S(1)} %fusion.42), channel_id=1, source_target_pairs={{0,16},{8,24},{16,0},{24,8},{1,17},{9,25},{17,1},{25,9},{2,18},{10... | collective-permute-start | bytes 1622024 | tf_op jit(solution)/shard_map/ppermute | solution.py:336
  113.1 0.8 copy-start.7
  113.1 2.0 copy-start.12
  115.1 25.0 %collective-permute-start.3 = (bf16[2,704,384]{2,1,0:T(8,128)(2,1)}, bf16[2,704,384]{2,1,0:T(8,128)(2,1)}, u32[]{:S(2)}, u32[]{:S(2)}) collective-permute-start(bf16[2,704,384]{2,1,0:T(8,128)(2,1)} %maximum_bitcast_fusion), channel_id=1, source_target_pairs={{0,8},{8,0},{16,24},{24,16},{1,9},{9,1},{17,25},{25,17},{2,10},{10... | collective-permute-start | bytes 3244040 | tf_op jit(solution)/shard_map/ppermute | solution.py:336
  123.3 16.7 %copy-start.8 = (bf16[1,1,704,384]{3,2,1,0:T(8,128)(2,1)S(1)}, bf16[1,1,704,384]{3,2,1,0:T(8,128)(2,1)}, u32[]{:S(2)}) copy-start(bf16[1,1,704,384]{3,2,1,0:T(8,128)(2,1)} %copy-done.7) | copy-start | bytes 1622020
  153.7 4.4 %copy-start.9 = (bf16[1,384,512]{2,1,0:T(8,128)(2,1)S(1)}, bf16[1,384,512]{2,1,0:T(8,128)(2,1)}, u32[]{:S(2)}) copy-start(bf16[1,384,512]{2,1,0:T(8,128)(2,1)} %get-tuple-element.23) | copy-start | bytes 1179652
  153.7 33.6 %all-to-all-start = ((bf16[8,192,512]{2,1,0:T(8,128)(2,1)}), bf16[8,192,512]{2,1,0:T(8,128)(2,1)}, u32[]{:S(2)}, u32[]{:S(2)}) async-start(bf16[8,192,512]{2,1,0:T(8,128)(2,1)} %pad_maximum_fusion), calls=%async_computation | async-start | bytes 3145728 | tf_op jit(solution)/shard_map/all_to_all | solution.py:437
  160.1 23.5 %collective-permute-start = (bf16[2,384,512]{2,1,0:T(8,128)(2,1)}, bf16[2,384,512]{2,1,0:T(8,128)(2,1)}, u32[]{:S(2)}, u32[]{:S(2)}) collective-permute-start(bf16[2,384,512]{2,1,0:T(8,128)(2,1)} %pad_maximum_fusion.2), channel_id=1, source_target_pairs={{0,8},{8,0},{16,24},{24,16},{1,9},{9,1},{17,25},{25,17},{2,10},{10... | collective-permute-start | bytes 2359304 | tf_op jit(solution)/shard_map/ppermute | solution.py:336
  186.8 20.6 %collective-permute-start.1 = (bf16[1,384,512]{2,1,0:T(8,128)(2,1)}, bf16[1,384,512]{2,1,0:T(8,128)(2,1)S(1)}, u32[]{:S(2)}, u32[]{:S(2)}) collective-permute-start(bf16[1,384,512]{2,1,0:T(8,128)(2,1)} %fusion.65), channel_id=1, source_target_pairs={{0,16},{8,24},{16,0},{24,8},{1,17},{9,25},{17,1},{25,9},{2,18},{10... | collective-permute-start | bytes 1179656 | tf_op jit(solution)/shard_map/ppermute | solution.py:336
  187.3 20.2 %copy-start.6 = (f32[384,2048]{1,0:T(8,128)S(1)}, f32[384,2048]{1,0:T(8,128)}, u32[]{:S(2)}) copy-start(f32[384,2048]{1,0:T(8,128)} %fusion.53) | copy-start | bytes 9437188

commit v2 on v1

--- a/solution.py
+++ b/solution.py
@@ -55,11 +55,13 @@
     su_ref,
     sd_ref,
     chosen_ref,
+    ids_ref,
     sg_out,
     su_out,
     sd_out,
     own_out,
     used_out,
+    ids_out,
     tok_all,
     sel,
     total,
@@ -97,15 +99,22 @@
         return out.at[rows, pl.ds(pl.multiple_of(block * cols, cols), cols)]
 
     def sources(w):
-        return [tok_ref, sg_ref, su_ref, sd_ref][w]
+        return [tok_ref, sg_ref, su_ref, sd_ref, ids_ref][w]
+
+    def halves(w):
+        return (0, 1) if w < 4 else (0,)
 
     def own_piece(w, h):
         ref = sources(w)
+        if w == 4:
+            return ref
         half = ref.shape[0] // 2
         return ref.at[pl.ds(h * half, half), :]
 
     def piece(w, block, h):
         ref = sources(w)
+        if w == 4:
+            return ids_out.at[block]
         half = ref.shape[0] // 2
         if w == 0:
             return tok_all.at[block, pl.ds(h * half, half), :]
@@ -136,12 +145,12 @@
 
     def ep_start(w):
         for position in range(len(orders[0])):
-            for h in (0, 1):
+            for h in halves(w):
                 ep_copy(w, h, 0, orders[h][position]).start()
 
     def ep_level(w, masks):
         for mask in masks:
-            for h in (0, 1):
+            for h in halves(w):
                 ep_arrival(w, h, mask).wait_recv()
                 for hop in later_hops(mask, orders[h]):
                     ep_copy(w, h, mask, hop).start()
@@ -178,7 +187,7 @@
         return [b for b in bits_below(split) if b > low]
 
     def local_copies():
-        items = [(0, tok_ref, tok_all.at[ep]), (1, tok_ref, columns(own_out, tp))]
+        items = [(0, tok_ref, tok_all.at[ep]), (6, ids_ref, ids_out.at[ep]), (1, tok_ref, columns(own_out, tp))]
         pairs = ((sg_ref, sg_out), (su_ref, su_out), (sd_ref, sd_out))
         for i, (ref, out) in enumerate(pairs):
             items.append((2 + i, ref, block_of(out, ep, pl.ds(0, ref.shape[0]))))
@@ -191,7 +200,7 @@
         copy.start()
     ep_levels = levels(n_ep)
     ep_level(0, ep_levels[0])
-    for w in (1, 2, 3):
+    for w in (1, 2, 3, 4):
         ep_start(w)
     for masks in ep_levels[1:]:
         ep_level(0, masks)
@@ -216,7 +225,7 @@
     own_used = pltpu.make_async_copy(sel.at[slot], columns(used_out, tp), local_sem.at[5])
     own_used.start()
 
-    for w in (1, 2, 3):
+    for w in (1, 2, 3, 4):
         ep_level(w, ep_levels[0])
     for mask in high_masks:
         disp_wait(
@@ -235,7 +244,7 @@
             for hop in later_hops(mask, tp_order):
                 tp_copy(mask, hop).start()
     for masks in ep_levels[1:]:
-        for w in (1, 2, 3):
+        for w in (1, 2, 3, 4):
             ep_level(w, masks)
     for mask in range(1, n_tp):
         if mask not in high_masks:
@@ -251,8 +260,8 @@
     for copy in locals_started[1:]:
         copy.wait()
     own_used.wait()
-    for w in range(4):
-        for h in (0, 1):
+    for w in range(5):
+        for h in halves(w):
             for mask in range(n_ep):
                 for hop in later_hops(mask, orders[h]):
                     ep_copy(w, h, mask, hop).wait_send()
@@ -299,25 +308,26 @@
             joined(shared_down),
             jax.ShapeDtypeStruct((n_tok, n_tp * width), bf16),
             jax.ShapeDtypeStruct((cap, n_tp * width), bf16),
+            jax.ShapeDtypeStruct((n_ep, n_exp, cap), jnp.int32),
         ),
-        in_specs=[vmem] * 5,
-        out_specs=(hbm,) * 5,
+        in_specs=[vmem] * 6,
+        out_specs=(hbm,) * 5 + (vmem,),
         scratch_shapes=[
             pltpu.VMEM((n_ep, n_tok, width), bf16),
             pltpu.VMEM((n_exp, cap, width), bf16),
             pltpu.VMEM((cap, width), jnp.float32),
-            pltpu.SemaphoreType.DMA((4, 2, n_ep)),
-            pltpu.SemaphoreType.DMA((4, 2, n_ep)),
+            pltpu.SemaphoreType.DMA((5, 2, n_ep)),
+            pltpu.SemaphoreType.DMA((5, 2, n_ep)),
             pltpu.SemaphoreType.DMA((n_tp,)),
             pltpu.SemaphoreType.DMA((n_tp,)),
             pltpu.SemaphoreType.DMA((n_tp,)),
             pltpu.SemaphoreType.DMA((n_tp,)),
-            pltpu.SemaphoreType.DMA((6,)),
+            pltpu.SemaphoreType.DMA((7,)),
         ],
         compiler_params=pltpu.CompilerParams(
             collective_id=0, has_side_effects=True, vmem_limit_bytes=48 * 1024 * 1024
         ),
-    )(tokens, shared_gate, shared_up, shared_down, chosen[:, :, None])
+    )(tokens, shared_gate, shared_up, shared_down, chosen[:, :, None], chosen)
 
 
 def flat_weight(weight):
@@ -332,34 +342,241 @@
     return (widened * inv_scale * gain).astype(jnp.bfloat16)
 
 
-def swap_tp(value, n_tp, mask):
-    return lax.ppermute(value, "tp", [(i, i ^ mask) for i in range(n_tp)])
-
-
-def gather_tp(block, n_tp):
+def finish_kernel(
+    n_tp,
+    n_ep,
+    part_ref,
+    normed_ref,
+    sg_hbm,
+    su_hbm,
+    sd_hbm,
+    down_hbm,
+    gates_ref,
+    place_ref,
+    ids_ref,
+    out_ref,
+    sg_ref,
+    su_ref,
+    sd_ref,
+    down_ref,
+    hidden,
+    acc,
+    parts,
+    parts_in,
+    stage,
+    back,
+    load_sem,
+    hid_send,
+    hid_recv,
+    sum_send,
+    sum_recv,
+    ret_send,
+    ret_recv,
+):
     tp = lax.axis_index("tp")
-    held = block[None]
-    for bit in bits_below(n_tp)[::-1]:
-        other = swap_tp(held, n_tp, bit)
-        upper = (tp // bit) % 2 == 1
-        first = jnp.where(upper, other, held)
-        second = jnp.where(upper, held, other)
-        held = jnp.stack([first, second], axis=1).reshape((-1,) + block.shape)
-    return held
-
-
-def scatter_sum_tp(partial, n_tp):
-    tp = lax.axis_index("tp")
-    rows = partial.shape[0]
-    width = partial.shape[1] // n_tp
-    blocks = [partial[:, i * width : (i + 1) * width] for i in range(n_tp)]
-    for bit in bits_below(n_tp):
-        upper = (tp // bit) % 2 == 1
-        send = [jnp.where(upper, blocks[i], blocks[i + 1]) for i in range(0, len(blocks), 2)]
-        keep = [jnp.where(upper, blocks[i + 1], blocks[i]) for i in range(0, len(blocks), 2)]
-        got = swap_tp(jnp.stack(send).astype(jnp.bfloat16), n_tp, bit)
-        blocks = [k + got[i].astype(jnp.float32) for i, k in enumerate(keep)]
-    return blocks[0]
+    ep = lax.axis_index("ep")
+    n_tok, width = out_ref.shape
+    n_exp = gates_ref.shape[0]
+    split = n_tp // n_exp
+    f32, bf16 = jnp.float32, jnp.bfloat16
+    order = bits_below(n_tp)[::-1]
+    half = part_ref.shape[0] // 2
+
+    barrier = pltpu.get_barrier_semaphore()
+    for mask in range(1, n_tp):
+        pl.semaphore_signal(barrier, inc=1, device_id={"tp": flip(tp, mask)}, device_id_type=MESH)
+    for mask in range(1, n_ep):
+        pl.semaphore_signal(barrier, inc=1, device_id={"ep": flip(ep, mask)}, device_id_type=MESH)
+    pl.semaphore_wait(barrier, n_tp + n_ep - 2)
+
+    def hid_copy(mask, hop, h):
+        rows = pl.ds(h * half, half)
+        block = flip(tp, mask)
+        return pltpu.make_async_remote_copy(
+            src_ref=part_ref.at[rows, :] if mask == 0 else hidden.at[block, rows, :],
+            dst_ref=hidden.at[block, rows, :],
+            send_sem=hid_send.at[mask | hop, h],
+            recv_sem=hid_recv.at[mask | hop, h],
+            device_id={"tp": flip(tp, hop)},
+            device_id_type=MESH,
+        )
+
+    def hid_arrived(mask, h):
+        dst = hidden.at[flip(tp, mask), pl.ds(h * half, half), :]
+        pltpu.make_async_remote_copy(
+            src_ref=dst,
+            dst_ref=dst,
+            send_sem=hid_send.at[mask, h],
+            recv_sem=hid_recv.at[mask, h],
+            device_id={"tp": flip(tp, mask)},
+            device_id_type=MESH,
+        ).wait_recv()
+
+    def sum_copy(mask):
+        return pltpu.make_async_remote_copy(
+            src_ref=parts.at[flip(tp, mask)],
+            dst_ref=parts_in.at[mask],
+            send_sem=sum_send.at[mask],
+            recv_sem=sum_recv.at[mask],
+            device_id={"tp": flip(tp, mask)},
+            device_id_type=MESH,
+        )
+
+    def ret_copy(mask):
+        return pltpu.make_async_remote_copy(
+            src_ref=stage.at[flip(ep, mask)],
+            dst_ref=back.at[ep],
+            send_sem=ret_send.at[mask],
+            recv_sem=ret_recv.at[mask],
+            device_id={"ep": flip(ep, mask)},
+            device_id_type=MESH,
+        )
+
+    def ret_arrived(mask):
+        dst = back.at[flip(ep, mask)]
+        pltpu.make_async_remote_copy(
+            src_ref=dst,
+            dst_ref=dst,
+            send_sem=ret_send.at[mask],
+            recv_sem=ret_recv.at[mask],
+            device_id={"ep": flip(ep, mask)},
+            device_id_type=MESH,
+        ).wait_recv()
+
+    for hop in order:
+        for h in (0, 1):
+            hid_copy(0, hop, h).start()
+    pairs = ((sg_hbm, sg_ref), (su_hbm, su_ref), (sd_hbm, sd_ref), (down_hbm, down_ref))
+    loads = [pltpu.make_async_copy(s, d, load_sem.at[i]) for i, (s, d) in enumerate(pairs)]
+    for load in loads:
+        load.start()
+
+    for load in loads[:3]:
+        load.wait()
+    chunk = n_tok // 2
+
+    def shared_rows(i, carry):
+        rows = pl.ds(pl.multiple_of(i * chunk, chunk), chunk)
+        x = normed_ref[rows, :]
+        contract = (((1,), (1,)), ((), ()))
+        gate = lax.dot_general(x, sg_ref[...], contract, preferred_element_type=f32)
+        up = lax.dot_general(x, su_ref[...], contract, preferred_element_type=f32)
+        mid = (jax.nn.silu(gate) * up).astype(bf16)
+        for block in range(n_tp):
+            cols = pl.ds(block * width, width)
+            parts[block, rows, :] = jnp.dot(
+                mid, sd_ref[:, cols], preferred_element_type=f32
+            ).astype(bf16)
+        return carry
+
+    lax.fori_loop(0, 2, shared_rows, 0)
+    loads[3].wait()
+
+    acc[...] = jnp.zeros_like(acc)
+
+    def add_block(mask):
+        block = flip(tp, mask)
+        value = part_ref[...] if mask == 0 else hidden[block]
+        slot = block // split
+        acc[slot] += lax.dot_general(
+            value, down_ref[block], (((0,), (0,)), ((), ())), preferred_element_type=f32
+        )
+
+    arrivals = sorted(
+        range(1, n_tp), key=lambda m: [order.index(b) for b in order if m & b][::-1]
+    )
+    tp_masks = list(range(1, n_tp))
+    first_hop = [m for m in arrivals if m == order[0]]
+    for mask in first_hop:
+        for h in (0, 1):
+            hid_arrived(mask, h)
+            for hop in later_hops(mask, order):
+                hid_copy(mask, hop, h).start()
+    for mask in tp_masks:
+        sum_copy(mask).start()
+    add_block(0)
+    for mask in first_hop:
+        add_block(mask)
+    for mask in arrivals:
+        if mask in first_hop:
+            continue
+        for h in (0, 1):
+            hid_arrived(mask, h)
+            for hop in later_hops(mask, order):
+                hid_copy(mask, hop, h).start()
+        add_block(mask)
+
+    slots = stage.shape[0] * stage.shape[2]
+    for s in range(n_exp):
+        weighted = (gates_ref[s] * acc[s]).astype(bf16)
+        cap = weighted.shape[0]
+        placer = lax.broadcasted_iota(jnp.int32, (slots, cap), 0) == place_ref[s]
+        placer = jnp.where(placer, 1.0, 0.0).astype(bf16)
+        placed = jnp.dot(placer, weighted, preferred_element_type=f32)
+        stage[:, s] = placed.reshape(stage.shape[0], stage.shape[2], width).astype(bf16)
+    ep_masks = sorted(range(1, n_ep), key=lambda m: -bin(m >> 1).count("1"))
+    for mask in ep_masks:
+        ret_copy(mask).start()
+    back[ep] = stage[ep]
+
+    ids = ids_ref[...]
+    picker = lax.broadcasted_iota(jnp.int32, (n_tok, ids.shape[1]), 0) == ids
+    picker = jnp.where(picker, 1.0, 0.0).astype(bf16)
+    for mask in ep_masks:
+        ret_arrived(mask)
+    acc[0] = jnp.dot(picker, back[...].reshape(-1, width), preferred_element_type=f32)
+    acc[0] += parts[tp].astype(f32)
+    for mask in tp_masks:
+        sum_copy(mask).wait_recv()
+        acc[0] += parts_in[mask].astype(f32)
+    out_ref[...] = acc[0].astype(bf16)
+
+    for mask in [0] + arrivals:
+        for hop in later_hops(mask, order):
+            for h in (0, 1):
+                hid_copy(mask, hop, h).wait_send()
+    for mask in tp_masks:
+        sum_copy(mask).wait_send()
+    for mask in ep_masks:
+        ret_copy(mask).wait_send()
+
+
+def finish(n_tp, n_ep, slot_most, hidden, normed, sg, su, sd, down, gates, place, ids):
+    n_tok = normed.shape[0]
+    width = down.shape[2]
+    n_exp, cap = gates.shape[:2]
+    vmem = pl.BlockSpec(memory_space=pltpu.VMEM)
+    hbm = pl.BlockSpec(memory_space=pl.ANY)
+    bf16 = jnp.bfloat16
+    dma = pltpu.SemaphoreType.DMA
+    return pl.pallas_call(
+        functools.partial(finish_kernel, n_tp, n_ep),
+        out_shape=jax.ShapeDtypeStruct((n_tok, width), bf16),
+        in_specs=[vmem, vmem, hbm, hbm, hbm, hbm, vmem, vmem, vmem],
+        out_specs=vmem,
+        scratch_shapes=[
+            pltpu.VMEM(sg.shape, bf16),
+            pltpu.VMEM(su.shape, bf16),
+            pltpu.VMEM(sd.shape, bf16),
+            pltpu.VMEM(down.shape, bf16),
+            pltpu.VMEM((n_tp,) + hidden.shape, bf16),
+            pltpu.VMEM((n_exp, cap, width), jnp.float32),
+            pltpu.VMEM((n_tp, n_tok, width), bf16),
+            pltpu.VMEM((n_tp, n_tok, width), bf16),
+            pltpu.VMEM((n_ep, n_exp, slot_most, width), bf16),
+            pltpu.VMEM((n_ep, n_exp, slot_most, width), bf16),
+            dma((4,)),
+            dma((n_tp, 2)),
+            dma((n_tp, 2)),
+            dma((n_tp,)),
+            dma((n_tp,)),
+            dma((n_ep,)),
+            dma((n_ep,)),
+        ],
+        compiler_params=pltpu.CompilerParams(
+            collective_id=1, has_side_effects=True, vmem_limit_bytes=56 * 1024 * 1024
+        ),
+    )(hidden, normed, sg, su, sd, down, gates, place, ids)
 
 
 def on_device(
@@ -381,11 +598,11 @@
     n_tok, width = tokens.shape
     f32 = jnp.float32
 
-    all_chosen = lax.all_gather(chosen, "ep", axis=0, tiled=True)
-    sg, su, sd, own_rows, used_rows = upfront(
+    sg, su, sd, own_rows, used_rows, all_chosen = upfront(
         n_tp, n_ep, tokens, shared_gate.T, shared_up.T, shared_down, chosen
     )
     sg, su, sd = flat_weight(sg), flat_weight(su), flat_weight(sd)
+    all_chosen = all_chosen.reshape(-1, cap)
 
     slot_most = 2 * cap // n_ep
     positions = jnp.arange(cap, dtype=jnp.int32)
@@ -413,33 +630,22 @@
     gate_values = jnp.einsum("hd,rd->hr", gate_weight, used, preferred_element_type=f32)
     up_values = jnp.einsum("hd,rd->hr", up_weight, used, preferred_element_type=f32)
     part_hidden = (jax.nn.silu(gate_values) * up_values).astype(jnp.bfloat16)
-    all_hidden = gather_tp(part_hidden, n_tp)
-
     normed = normalise(own_rows, norm_gain)
-    gate_sum = jnp.einsum("rd,hd->rh", normed, sg, preferred_element_type=f32)
-    up_sum = jnp.einsum("rd,hd->rh", normed, su, preferred_element_type=f32)
-    shared_hidden = (jax.nn.silu(gate_sum) * up_sum).astype(jnp.bfloat16)
-    partial_out = jnp.dot(shared_hidden, sd, preferred_element_type=f32)
-    shared_part = scatter_sum_tp(partial_out, n_tp)
-
-    hidden = all_hidden.reshape(n_exp, expert_down.shape[1], cap)
-    placed = []
-    for s in range(n_exp):
-        outputs = jnp.einsum("fr,fd->rd", hidden[s], expert_down[s], preferred_element_type=f32)
-        weighted = (gates[s][:, None] * outputs).astype(jnp.bfloat16)
-        placer = jnp.arange(n_ep * slot_most, dtype=jnp.int32)[:, None] == slot_index[s][None, :]
-        placed.append(
-            jnp.dot(placer.astype(jnp.bfloat16), weighted, preferred_element_type=f32)
-            .astype(jnp.bfloat16)
-            .reshape(n_ep, slot_most, width)
-        )
-    stacked = jnp.concatenate(placed, axis=1)
-    returned = lax.all_to_all(stacked, "ep", split_axis=0, concat_axis=0, tiled=True)
-    flat_values = returned.reshape(-1, width)
-    flat_ids = own_ids.reshape(-1)
-    picker = jnp.arange(n_tok, dtype=jnp.int32)[:, None] == flat_ids[None, :]
-    routed = jnp.dot(picker.astype(jnp.bfloat16), flat_values, preferred_element_type=f32)
-    return (shared_part + routed).astype(jnp.bfloat16)
+    down = expert_down.reshape(n_tp, -1, width)
+    return finish(
+        n_tp,
+        n_ep,
+        slot_most,
+        part_hidden,
+        normed,
+        sg,
+        su,
+        sd,
+        down,
+        gates[:, :, None],
+        slot_index[:, None, :],
+        own_ids.reshape(1, -1),
+    )
 
 
 def solution(mesh):

time: 211 us -> 166 us (0.79)
  Pallas kernels: 75.3 us -> 146 us
  waiting for transfers between devices: 49.4 us -> 0 us
  matrix products: 27.1 us -> 4.38 us
  blocking collectives: 21.9 us -> 0 us
  other arithmetic: 21 us -> 5.15 us
  starting transfers between devices: 8.7 us -> 0 us
  local copies, waits for them, and re-layouts: 6.25 us -> 9.86 us
    pallas_call x0 -> x1, Pallas kernels: none -> 70.4 us  [finish(): pl.pallas_call(functools.partial(finish_kernel, n_tp, n_ep), out_shape=ja...]
    ppermute x4 -> x0, waiting for transfers between devices: 49.4 us -> none  [swap_tp(): return lax.ppermute(value, 'tp', [(i, i ^ mask) for i in range(n_tp)])]
    dot_general x5 -> x0, matrix products: 23.4 us -> none  [the longest x1 8.23 us: on_device(): partial_out = jnp.dot(shared_hidden, sd, preferred_element_type=f32)]
    all_gather x1 -> x0, blocking collectives: 21.9 us -> none  [on_device(): all_chosen = lax.all_gather(chosen, 'ep', axis=0, tiled=True)]
    another operation x5 -> x0, other arithmetic: 9.31 us -> none  [the longest x2 4.88 us: scatter_sum_tp(): got = swap_tp(jnp.stack(send).astype(jnp.bfloat16), n_tp, bit)]
    all_to_all x1 -> x0, starting transfers between devices: 4.44 us -> none  [on_device(): lax.all_to_all(stacked, 'ep', split_axis=0, concat_axis=0, tiled=True)]
    ppermute x4 -> x0, starting transfers between devices: 4.27 us -> none  [swap_tp(): return lax.ppermute(value, 'tp', [(i, i ^ mask) for i in range(n_tp)])]
    convert_element_type x2 -> x1, other arithmetic: 5.72 us -> 3.05 us  [normalise(): return (widened * inv_scale * gain).astype(jnp.bfloat16)]
  transfers between devices with their start and end apart: 5 -> 0, of which waited for: 3 -> 0; matrix products, arithmetic and copies ran while one was open for 12% -> 0% of each run, Pallas kernels for 0% -> 0%
where the time goes in v2:
time: 166 us
  Pallas kernels  146 us (88%)
  local copies, waits for them, and re-layouts  9.86 us (6%)
  other arithmetic  5.15 us (3%)
  matrix products  4.38 us (3%)
    pallas_call x1, Pallas kernels, upfront(): pl.pallas_call(functools.partial(gather_kernel, n_tp, n_ep), out_shape=(j...  75.7 us
    pallas_call x1, Pallas kernels, finish(): pl.pallas_call(functools.partial(finish_kernel, n_tp, n_ep), out_shape=ja...  70.4 us
    unnamed x23, local copies, waits for them, and re-layouts  6.45 us

profile of v2, /device:TPU:0, one launch (start us, length us, event | category | flops | bytes accessed | tf_op | source)
XLA Modules:
  0.0 165.6 jit_solution(17624350733928128641)
XLA Ops:
  0.0 0.0 copy-start
  0.0 1.0 copy.13.chosen_ref
  1.0 0.0 copy-start.2
  1.0 1.0 copy-done.2
  2.0 1.0 copy-done.3
  3.0 1.0 copy-done.4
  4.0 1.0 copy-done.5
  5.0 0.7 copy-done.6
  5.7 75.7 %shard_map.100 = (bf16[704,2048]{1,0:T(8,128)(2,1)}, bf16[704,2048]{1,0:T(8,128)(2,1)}, bf16[704,2048]{1,0:T(8,128)(2,1)}, bf16[384,2048]{1,0:T(8,128)(2,1)S(1)}...) custom-call(bf16[384,512]{1,0:T(8,128)(2,1)S(1)} %copy-done.2, bf16[704,256]{1,0:T(8,128)(2,1)S(1)} %bitcast.27, ...), custom_call_target="tpu_custom_call" | custom-call | tf_op jit(solution)/shard_map/pallas_call | solution.py:303
  81.4 0.0 copy-start.1
  81.4 0.7 fusion
  82.1 0.0 copy-done
  82.1 0.0 copy-done.8
  82.1 0.0 copy-start.10
  82.1 1.8 %fusion.10 = f32[704,384]{1,0:T(8,128)S(1)} fusion(bf16[1,1,704,2048]{3,2,1,0:T(8,128)(2,1)S(1)} %copy-done, bf16[384,2048]{1,0:T(8,128)(2,1)S(1)} %get-tuple-element.11, f32[2048]{0:T(1024)S(1)} %copy-done.8, f32[384]{0:T(512)S(1)} %add_rsqrt_fusion.1), kind=kOutput, calls=%fused_computation.16 | convolution fusion | flops 1110441984 | bytes 5547520 | tf_op jit(solution)/shard_map/hd,rd->hr/dot_general | solution.py:630
  83.9 0.0 copy-done.1
  83.9 0.0 copy-done.10
  83.9 2.6 %fusion.19.part_ref = bf16[704,384]{1,0:T(8,128)(2,1)} fusion(bf16[1,1,704,2048]{3,2,1,0:T(8,128)(2,1)S(1)} %copy-done.10, f32[704,384]{1,0:T(8,128)S(1)} %fusion.10, bf16[384,2048]{1,0:T(8,128)(2,1)S(1)} %get-tuple-element.11, f32[2048]{0:T(1024)S(1)} %copy-done.8, f32[384]{0:T(512)S(1)} %add_rsqrt_fusion.1), kind=kOutput, calls=%fused_computation.19 | convolution fusion | flops 1112064000 | bytes 6088192 | tf_op jit(solution)/shard_map/hd,rd->hr/dot_general | solution.py:631
  86.5 0.3 fusion.24
  86.9 0.1 add.78
  87.0 0.1 lt.48
  87.0 0.1 compare_select_fusion
  87.2 0.7 select_reduce_fusion
  87.8 0.7 sub.28.ids_ref
  88.5 3.0 %fusion.5.normed_ref = bf16[384,2048]{1,0:T(8,128)(2,1)} fusion(bf16[384,2048]{1,0:T(8,128)(2,1)} %copy-done.1, f32[384]{0:T(512)S(1)} %add_rsqrt_fusion, f32[2048]{0:T(1024)S(1)} %copy-done.8), kind=kLoop, calls=%fused_computation.9 | loop fusion | flops 3145728 | bytes 3155456 | tf_op jit(solution)/shard_map/convert_element_type | solution.py:342
  91.6 0.0 copy-done.7
  91.6 0.3 convert_reduce_fusion
  91.9 0.6 broadcast_in_dim.24.place_ref
  92.5 0.0 copy-done.9
  92.5 0.9 copy.14.gates_ref
  93.4 70.4 %shard_map.101 = bf16[384,512]{1,0:T(8,128)(2,1)} custom-call(bf16[704,384]{1,0:T(8,128)(2,1)} %fusion.19.part_ref, bf16[384,2048]{1,0:T(8,128)(2,1)} %fusion.5.normed_ref, bf16[704,2048]{1,0:T(8,128)(2,1)} %get-tuple-element.13.sg_hbm, bf16[704,2048]{1,0:T(8,128)(2,1)} %get-tuple-element.14.su_hbm, bf16[704,2048]{1,0:T(8,128)(2,1)} %get-tuple-element.15.sd_hbm, ...), custom_call_target="tpu_custom_call" | custom-call | tf_op jit(solution)/shard_map/pallas_call | solution.py:552
  163.9 1.8 %copy.16 = bf16[384,512]{1,0:T(8,128)(2,1)} copy(bf16[384,512]{1,0:T(8,128)(2,1)} %shard_map.101) | data formatting | bytes 786432
  (13 shorter events, 0.1 us)
Async XLA Ops:
  0.0 82.1 %copy-start = (bf16[1,1,704,2048]{3,2,1,0:T(8,128)(2,1)S(1)}, bf16[1,1,704,2048]{3,2,1,0:T(8,128)(2,1)}, u32[]{:S(2)}) copy-start(bf16[1,1,704,2048]{3,2,1,0:T(8,128)(2,1)} %param.15) | copy-start | bytes 8650756
  1.0 1.0 copy-start.2
  2.0 1.0 copy-start.3
  3.0 1.0 copy-start.4
  4.0 1.0 copy-start.5
  5.0 0.7 copy-start.6
  5.7 76.4 %copy-start.8 = (f32[2048]{0:T(1024)S(1)}, f32[2048]{0:T(1024)}, u32[]{:S(2)}) copy-start(f32[2048]{0:T(1024)} %param.11) | copy-start | bytes 24580
  81.4 2.5 %copy-start.1 = (bf16[384,2048]{1,0:T(8,128)(2,1)}, bf16[384,2048]{1,0:T(8,128)(2,1)S(1)}, u32[]{:S(2)}) copy-start(bf16[384,2048]{1,0:T(8,128)(2,1)S(1)} %get-tuple-element.12) | copy-start | bytes 4718596
  82.1 1.8 %copy-start.10 = (bf16[1,1,704,2048]{3,2,1,0:T(8,128)(2,1)S(1)}, bf16[1,1,704,2048]{3,2,1,0:T(8,128)(2,1)}, u32[]{:S(2)}) copy-start(bf16[1,1,704,2048]{3,2,1,0:T(8,128)(2,1)} %param.16) | copy-start | bytes 8650756
  86.5 5.0 %copy-start.7 = (s32[2,384]{1,0:T(2,128)S(1)}, s32[2,384]{1,0:T(2,128)}, u32[]{:S(2)}) copy-start(s32[2,384]{1,0:T(2,128)} %ids_ref.1) | copy-start | bytes 9220
  86.5 6.0 %copy-start.9 = (f32[2,384]{1,0:T(2,128)S(1)}, f32[2,384]{1,0:T(2,128)}, u32[]{:S(2)}) copy-start(f32[2,384]{1,0:T(2,128)} %param.19) | copy-start | bytes 9220

commit v3 on v2

--- a/solution.py
+++ b/solution.py
@@ -168,19 +168,35 @@
             device_id_type=MESH,
         )
 
-    def disp_copy(mask, hop):
+    def used_piece(mask, h):
+        rows = pl.ds(h * (cap // 2), cap // 2)
+        cols = pl.ds(pl.multiple_of(flip(tp, mask) * width, width), width)
+        return used_out.at[rows, cols]
+
+    def disp_copy(mask, hop, h):
         if mask == 0:
-            src = sel.at[flip(tp, hop) // split]
+            src = sel.at[flip(tp, hop) // split, pl.ds(h * (cap // 2), cap // 2), :]
         else:
-            src = columns(used_out, flip(tp, mask))
+            src = used_piece(mask, h)
         return pltpu.make_async_remote_copy(
             src_ref=src,
-            dst_ref=columns(used_out, flip(tp, mask)),
-            send_sem=disp_send.at[mask | hop],
-            recv_sem=disp_recv.at[mask | hop],
+            dst_ref=used_piece(mask, h),
+            send_sem=disp_send.at[mask | hop, h],
+            recv_sem=disp_recv.at[mask | hop, h],
             device_id={"tp": flip(tp, hop)},
             device_id_type=MESH,
         )
+
+    def disp_arrival(mask, h):
+        dst = used_piece(mask, h)
+        pltpu.make_async_remote_copy(
+            src_ref=dst,
+            dst_ref=dst,
+            send_sem=disp_send.at[mask, h],
+            recv_sem=disp_recv.at[mask, h],
+            device_id={"tp": flip(tp, mask)},
+            device_id_type=MESH,
+        ).wait_recv()
 
     def low_hops(mask):
         low = mask % split
@@ -194,7 +210,8 @@
         return [pltpu.make_async_copy(s, d, local_sem.at[i]) for i, s, d in items]
 
     ep_start(0)
-    tp_copy(0, tp_order[0]).start()
+    for hop in tp_order:
+        tp_copy(0, hop).start()
     locals_started = local_copies()
     for copy in locals_started:
         copy.start()
@@ -218,23 +235,19 @@
         lax.fori_loop(0, n_ep, add_source, 0)
         sel[s] = total[...].astype(jnp.bfloat16)
 
-    for mask in high_masks:
-        disp_copy(0, mask).start()
-    for hop in low_hops(0):
-        disp_copy(0, hop).start()
+    for hop in high_masks + low_hops(0):
+        for h in (0, 1):
+            disp_copy(0, hop, h).start()
     own_used = pltpu.make_async_copy(sel.at[slot], columns(used_out, tp), local_sem.at[5])
     own_used.start()
 
     for w in (1, 2, 3, 4):
         ep_level(w, ep_levels[0])
     for mask in high_masks:
-        disp_wait(
-            columns(used_out, flip(tp, mask)), disp_send, disp_recv, mask, tp
-        )
-        for hop in low_hops(mask):
-            disp_copy(mask, hop).start()
-    for hop in tp_order[1:]:
-        tp_copy(0, hop).start()
+        for h in (0, 1):
+            disp_arrival(mask, h)
+            for hop in low_hops(mask):
+                disp_copy(mask, hop, h).start()
     tp_seen = []
     for mask in sorted(range(1, n_tp), key=lambda m: [tp_order.index(b) for b in tp_order if m & b][-1]):
         last = [b for b in tp_order if mask & b][-1]
@@ -248,9 +261,10 @@
             ep_level(w, masks)
     for mask in range(1, n_tp):
         if mask not in high_masks:
-            disp_wait(columns(used_out, flip(tp, mask)), disp_send, disp_recv, mask, tp)
-            for hop in low_hops(mask):
-                disp_copy(mask, hop).start()
+            for h in (0, 1):
+                disp_arrival(mask, h)
+                for hop in low_hops(mask):
+                    disp_copy(mask, hop, h).start()
     for mask in sorted(range(1, n_tp), key=lambda m: [tp_order.index(b) for b in tp_order if m & b][-1]):
         if mask not in tp_seen:
             disp_wait(columns(own_out, flip(tp, mask)), tp_send, tp_recv, mask, tp)
@@ -273,7 +287,8 @@
         if mask == 0:
             hops = high_masks + hops
         for hop in hops:
-            disp_copy(mask, hop).wait_send()
+            for h in (0, 1):
+                disp_copy(mask, hop, h).wait_send()
 
 
 def disp_wait(dst, send_sem, recv_sem, mask, tp):
@@ -310,7 +325,7 @@
             jax.ShapeDtypeStruct((cap, n_tp * width), bf16),
             jax.ShapeDtypeStruct((n_ep, n_exp, cap), jnp.int32),
         ),
-        in_specs=[vmem] * 6,
+        in_specs=[vmem] + [hbm] * 3 + [vmem] * 2,
         out_specs=(hbm,) * 5 + (vmem,),
         scratch_shapes=[
             pltpu.VMEM((n_ep, n_tok, width), bf16),
@@ -320,8 +335,8 @@
             pltpu.SemaphoreType.DMA((5, 2, n_ep)),
             pltpu.SemaphoreType.DMA((n_tp,)),
             pltpu.SemaphoreType.DMA((n_tp,)),
-            pltpu.SemaphoreType.DMA((n_tp,)),
-            pltpu.SemaphoreType.DMA((n_tp,)),
+            pltpu.SemaphoreType.DMA((n_tp, 2)),
+            pltpu.SemaphoreType.DMA((n_tp, 2)),
             pltpu.SemaphoreType.DMA((7,)),
         ],
         compiler_params=pltpu.CompilerParams(

time: 166 us -> 157 us (0.946)
  Pallas kernels: 146 us -> 136 us
    pallas_call x1, Pallas kernels: 75.7 us -> 67.2 us  [upfront(): pl.pallas_call(functools.partial(gather_kernel, n_tp, n_ep), out_shape=(j...]
where the time goes in v3:
time: 157 us; the launch traced here: 156 us
  Pallas kernels  136 us (87%)
  local copies, waits for them, and re-layouts  9.86 us (6%)
  other arithmetic  5.15 us (3%)
  matrix products  4.38 us (3%)
    pallas_call x1, Pallas kernels, finish(): pl.pallas_call(functools.partial(finish_kernel, n_tp, n_ep), out_shape=ja...  69.2 us
    pallas_call x1, Pallas kernels, upfront(): pl.pallas_call(functools.partial(gather_kernel, n_tp, n_ep), out_shape=(j...  67.2 us
    unnamed x23, local copies, waits for them, and re-layouts  6.46 us

profile of v3, /device:TPU:0, one launch (start us, length us, event | category | flops | bytes accessed | tf_op | source)
XLA Modules:
  0.0 155.8 jit_solution(2990141676249425929)
XLA Ops:
  0.0 0.0 copy-start
  0.0 1.0 copy.13.chosen_ref
  1.0 0.0 copy-start.2
  1.0 1.0 copy-done.2
  2.0 1.0 copy-done.3
  3.0 1.0 copy-done.4
  4.0 1.0 copy-done.5
  5.0 0.7 copy-done.6
  5.7 67.2 %shard_map.100 = (bf16[704,2048]{1,0:T(8,128)(2,1)}, bf16[704,2048]{1,0:T(8,128)(2,1)}, bf16[704,2048]{1,0:T(8,128)(2,1)}, bf16[384,2048]{1,0:T(8,128)(2,1)S(1)}...) custom-call(bf16[384,512]{1,0:T(8,128)(2,1)S(1)} %copy-done.2, bf16[704,256]{1,0:T(8,128)(2,1)S(1)} %bitcast.27, ...), custom_call_target="tpu_custom_call" | custom-call | tf_op jit(solution)/shard_map/pallas_call | solution.py:318
  72.8 0.0 copy-start.1
  72.8 0.7 fusion
  73.5 0.0 copy-done
  73.5 0.0 copy-done.8
  73.5 0.0 copy-start.10
  73.6 1.8 %fusion.10 = f32[704,384]{1,0:T(8,128)S(1)} fusion(bf16[1,1,704,2048]{3,2,1,0:T(8,128)(2,1)S(1)} %copy-done, bf16[384,2048]{1,0:T(8,128)(2,1)S(1)} %get-tuple-element.11, f32[2048]{0:T(1024)S(1)} %copy-done.8, f32[384]{0:T(512)S(1)} %add_rsqrt_fusion.1), kind=kOutput, calls=%fused_computation.16 | convolution fusion | flops 1110441984 | bytes 5547520 | tf_op jit(solution)/shard_map/hd,rd->hr/dot_general | solution.py:645
  75.3 0.0 copy-done.1
  75.3 0.0 copy-done.10
  75.4 2.6 %fusion.19.part_ref = bf16[704,384]{1,0:T(8,128)(2,1)} fusion(bf16[1,1,704,2048]{3,2,1,0:T(8,128)(2,1)S(1)} %copy-done.10, f32[704,384]{1,0:T(8,128)S(1)} %fusion.10, bf16[384,2048]{1,0:T(8,128)(2,1)S(1)} %get-tuple-element.11, f32[2048]{0:T(1024)S(1)} %copy-done.8, f32[384]{0:T(512)S(1)} %add_rsqrt_fusion.1), kind=kOutput, calls=%fused_computation.19 | convolution fusion | flops 1112064000 | bytes 6088192 | tf_op jit(solution)/shard_map/hd,rd->hr/dot_general | solution.py:646
  78.0 0.3 fusion.24
  78.3 0.1 add.78
  78.4 0.1 lt.48
  78.5 0.1 compare_select_fusion
  78.6 0.7 select_reduce_fusion
  79.3 0.7 sub.28.ids_ref
  80.0 3.0 %fusion.5.normed_ref = bf16[384,2048]{1,0:T(8,128)(2,1)} fusion(bf16[384,2048]{1,0:T(8,128)(2,1)} %copy-done.1, f32[384]{0:T(512)S(1)} %add_rsqrt_fusion, f32[2048]{0:T(1024)S(1)} %copy-done.8), kind=kLoop, calls=%fused_computation.9 | loop fusion | flops 3145728 | bytes 3155456 | tf_op jit(solution)/shard_map/convert_element_type | solution.py:357
  83.0 0.0 copy-done.7
  83.0 0.3 convert_reduce_fusion
  83.4 0.6 broadcast_in_dim.24.place_ref
  83.9 0.0 copy-done.9
  84.0 0.9 copy.14.gates_ref
  84.9 69.2 %shard_map.101 = bf16[384,512]{1,0:T(8,128)(2,1)} custom-call(bf16[704,384]{1,0:T(8,128)(2,1)} %fusion.19.part_ref, bf16[384,2048]{1,0:T(8,128)(2,1)} %fusion.5.normed_ref, bf16[704,2048]{1,0:T(8,128)(2,1)} %get-tuple-element.13.sg_hbm, bf16[704,2048]{1,0:T(8,128)(2,1)} %get-tuple-element.14.su_hbm, bf16[704,2048]{1,0:T(8,128)(2,1)} %get-tuple-element.15.sd_hbm, ...), custom_call_target="tpu_custom_call" | custom-call | tf_op jit(solution)/shard_map/pallas_call | solution.py:567
  154.1 1.8 %copy.16 = bf16[384,512]{1,0:T(8,128)(2,1)} copy(bf16[384,512]{1,0:T(8,128)(2,1)} %shard_map.101) | data formatting | bytes 786432
  (13 shorter events, 0.1 us)
Async XLA Ops:
  0.0 73.5 %copy-start = (bf16[1,1,704,2048]{3,2,1,0:T(8,128)(2,1)S(1)}, bf16[1,1,704,2048]{3,2,1,0:T(8,128)(2,1)}, u32[]{:S(2)}) copy-start(bf16[1,1,704,2048]{3,2,1,0:T(8,128)(2,1)} %param.15) | copy-start | bytes 8650756
  1.0 1.0 copy-start.2
  2.0 1.0 copy-start.3
  3.0 1.0 copy-start.4
  4.0 1.0 copy-start.5
  5.0 0.7 copy-start.6
  5.7 67.9 %copy-start.8 = (f32[2048]{0:T(1024)S(1)}, f32[2048]{0:T(1024)}, u32[]{:S(2)}) copy-start(f32[2048]{0:T(1024)} %param.11) | copy-start | bytes 24580
  72.8 2.5 %copy-start.1 = (bf16[384,2048]{1,0:T(8,128)(2,1)}, bf16[384,2048]{1,0:T(8,128)(2,1)S(1)}, u32[]{:S(2)}) copy-start(bf16[384,2048]{1,0:T(8,128)(2,1)S(1)} %get-tuple-element.12) | copy-start | bytes 4718596
  73.5 1.8 %copy-start.10 = (bf16[1,1,704,2048]{3,2,1,0:T(8,128)(2,1)S(1)}, bf16[1,1,704,2048]{3,2,1,0:T(8,128)(2,1)}, u32[]{:S(2)}) copy-start(bf16[1,1,704,2048]{3,2,1,0:T(8,128)(2,1)} %param.16) | copy-start | bytes 8650756
  78.0 5.0 %copy-start.7 = (s32[2,384]{1,0:T(2,128)S(1)}, s32[2,384]{1,0:T(2,128)}, u32[]{:S(2)}) copy-start(s32[2,384]{1,0:T(2,128)} %ids_ref.1) | copy-start | bytes 9220
  78.0 6.0 %copy-start.9 = (f32[2,384]{1,0:T(2,128)S(1)}, f32[2,384]{1,0:T(2,128)}, u32[]{:S(2)}) copy-start(f32[2,384]{1,0:T(2,128)} %param.19) | copy-start | bytes 9220
